TPU v7x, 512 devices: a whole 4x8x8 slice. The times are simulated.
512 devices in a mesh: dp: 16 (over y_lo, x), ctx: 32 (over y_hi, z, core).
Axes of the slice: x: 4, y: 8 (y_hi: 2, y_lo: 4; y = y_hi * 4 + y_lo), z: 8, core: 2. Of those that a mesh axis runs over, the one named last changes fastest.
Arguments:
- query_rows: bfloat16 [65536, 4096], P(('dp', 'ctx')), may hold values from -32 to 32
- key_rows: bfloat16 [65536, 512], P(('dp', 'ctx')), may hold values from -8 to 8
- value_rows: bfloat16 [65536, 512], P(('dp', 'ctx')), may hold values from -6 to 6
- out_grad: bfloat16 [65536, 4096], P(('dp', 'ctx')), may hold values from -24 to 24
- destination: int32 [16, 4096], P('dp'), may hold values from 0 to 4095, as said below
- group_first: int32 [16, 32], P('dp', 'ctx'), may hold values from 0 to 31, as said below
Outputs:
- attended: bfloat16 [65536, 4096], P(('dp', 'ctx'))
- grad_query: bfloat16 [65536, 4096], P(('dp', 'ctx'))
- grad_key: bfloat16 [65536, 512], P(('dp', 'ctx'))
- grad_value: bfloat16 [65536, 512], P(('dp', 'ctx'))
- bias_grad: float32 [4608], replicated
Inputs may be any that keep to these rules, and one draw needn't show every extreme that they name: For each replica r, destination[r] is a permutation of 0 to 4095. Of the 128 tokens of one index of ctx, at most 8 take slots in any one block, and in every replica some index and block reach 8. group_first[r, b] equals b where a sequence group begins (always at b = 0) and group_first[r, b - 1] otherwise.
All inputs are finite; a program needn't handle non-finite values.
Results may differ from a plain program's by a relative error of at most 0.008.
Values may be sent and summed in bfloat16 or wider, within the bound.
A program may use at most 64 MiB of HBM per device.

v0:
```python
import math

import jax
import jax.numpy as jnp
from jax import lax
from jax.sharding import PartitionSpec as P

HD = 128
GROUP = 8


def from_behind(shard, axis, by):
    count = lax.axis_size(axis)
    pairs = [(i, i + by) for i in range(count) if 0 <= i + by < count]
    return lax.ppermute(shard, axis, pairs)


def cut_along(shard, dim, count):
    before, after = (shard.shape[:dim], shard.shape[dim + 1 :])
    return jnp.moveaxis(shard.reshape(*before, count, -1, *after), dim, 0)


def sent_and_summed(shard, axis, dim):
    blocks = cut_along(shard, dim, lax.axis_size(axis))
    arrived = lax.all_to_all(blocks, axis, split_axis=0, concat_axis=0, tiled=True)
    return arrived.sum(axis=0)


def from_everyone(shard, axis):
    count = lax.axis_size(axis)
    return lax.all_to_all(
        jnp.broadcast_to(shard[None], (count, *shard.shape)), axis, 0, 0, tiled=True
    )


def taken_together(shard, axis):
    everything = from_everyone(shard, axis)
    return jnp.sum(everything, axis=0)


def joined_along(blocks, dim):
    shape = list(blocks.shape[1:])
    shape[dim] *= blocks.shape[0]
    return jnp.moveaxis(blocks, 0, dim).reshape(shape)


def collect(shard, axis, dim):
    blocks = from_everyone(shard, axis)
    return joined_along(blocks, dim)


def product(form, left, right):
    return jnp.einsum(form, left, right, preferred_element_type=jnp.float32)


def block_attention(query_own, keys_own, values_own, grads_own, keys_prior, values_prior, linked):
    length = query_own.shape[0]
    scaling = query_own.shape[-1] ** (-0.5)
    places = jnp.arange(length)
    lower_mask = places[:, None] >= places[None, :]
    upper_mask = jnp.logical_and(places[:, None] >= 0 * places[None, :], linked)
    score_own = jnp.where(
        lower_mask, product("qhgd,khd->hgqk", query_own, keys_own) * scaling, -jnp.inf
    )
    score_prior = jnp.where(
        upper_mask, product("qhgd,khd->hgqk", query_own, keys_prior) * scaling, -jnp.inf
    )
    ceiling = jnp.maximum(jnp.max(score_own, axis=-1), jnp.max(score_prior, axis=-1))[..., None]
    raw_own = jnp.exp(score_own - ceiling)
    raw_prior = jnp.exp(score_prior - ceiling)
    denom = jnp.sum(raw_own, axis=-1, keepdims=True) + jnp.sum(raw_prior, axis=-1, keepdims=True)
    prob_own = raw_own / denom
    prob_prior = raw_prior / denom
    weight_own = prob_own.astype(jnp.bfloat16)
    weight_prior = prob_prior.astype(jnp.bfloat16)
    attended = (
        product("hgqk,khd->qhgd", weight_own, values_own)
        + product("hgqk,khd->qhgd", weight_prior, values_prior)
    ).astype(jnp.bfloat16)
    press_own = product("qhgd,khd->hgqk", grads_own, values_own)
    press_prior = product("qhgd,khd->hgqk", grads_own, values_prior)
    centred = (jnp.sum(prob_own * press_own, axis=-1) + jnp.sum(prob_prior * press_prior, axis=-1))[
        ..., None
    ]
    slope_own = (prob_own * (press_own - centred) * scaling).astype(jnp.bfloat16)
    slope_prior = (prob_prior * (press_prior - centred) * scaling).astype(jnp.bfloat16)
    grad_q = (
        product("hgqk,khd->qhgd", slope_own, keys_own)
        + product("hgqk,khd->qhgd", slope_prior, keys_prior)
    ).astype(jnp.bfloat16)
    key_own = product("hgqk,qhgd->khd", slope_own, query_own).astype(jnp.bfloat16)
    key_prior = product("hgqk,qhgd->khd", slope_prior, query_own).astype(jnp.bfloat16)
    value_own = product("hgqk,qhgd->khd", weight_own, grads_own).astype(jnp.bfloat16)
    value_prior = product("hgqk,qhgd->khd", weight_prior, grads_own).astype(jnp.bfloat16)
    return (attended, grad_q, key_own, key_prior, value_own, value_prior)


def local(query_rows, key_rows, value_rows, out_grad, destination, group_first):
    length = query_rows.shape[0]
    devices = lax.axis_size("ctx")
    replicas = lax.axis_size("dp")
    own_index = lax.axis_index("ctx")
    capacity = 2 * length // devices
    slot_total = devices * capacity
    kv_heads = key_rows.shape[1] // HD
    wide = GROUP * HD
    plan = destination[0]
    blocks = (plan // length).reshape(devices, length)
    hits = (blocks[:, :, None] == jnp.arange(devices, dtype=jnp.int32)[None, None, :]).astype(
        jnp.int32
    )
    ranks = jnp.sum((jnp.cumsum(hits, axis=1) - hits) * hits, axis=2)
    flat_ranks = ranks.reshape(-1)
    inverse = jnp.zeros_like(plan).at[plan].set(jnp.arange(plan.shape[0], dtype=jnp.int32))
    my_target = lax.dynamic_index_in_dim(blocks, own_index, 0, keepdims=False)
    my_rank = lax.dynamic_index_in_dim(ranks, own_index, 0, keepdims=False)
    local_ids = jnp.arange(length, dtype=jnp.int32)
    send_place = my_target * capacity + my_rank
    linked = group_first[0, 0] < own_index

    def ordering(places):
        return jnp.full((slot_total,), length, jnp.int32).at[places].set(local_ids, mode="drop")

    def outgoing(rows, order, width):
        picked = jnp.take(rows, order, axis=0, mode="fill", fill_value=0)
        return picked.reshape(devices, capacity, kv_heads, width)

    def settle(buffer, places):
        flat = buffer.reshape((slot_total,) + buffer.shape[2:])
        return jnp.take(flat, places, axis=0, mode="fill", fill_value=0)

    def returning(rows, order, heads, width):
        picked = jnp.take(
            rows.reshape(length, heads, width), order, axis=0, mode="fill", fill_value=0
        )
        return picked.reshape(devices, capacity, heads, width)

    tokens_at = lax.dynamic_slice_in_dim(inverse, own_index * length, length)
    recv_place = tokens_at // length * capacity + flat_ranks[tokens_at]
    send_order = ordering(send_place)
    back_order = ordering(recv_place)
    queries = outgoing(query_rows, send_order, wide)
    keys_out = outgoing(key_rows, send_order, HD)
    values_out = outgoing(value_rows, send_order, HD)
    grads_out = outgoing(out_grad, send_order, wide)
    pieces = (
        lax.all_to_all(queries, "ctx", split_axis=0, concat_axis=0, tiled=True),
        lax.all_to_all(keys_out, "ctx", split_axis=0, concat_axis=0, tiled=True),
        lax.all_to_all(values_out, "ctx", split_axis=0, concat_axis=0, tiled=True),
        lax.all_to_all(grads_out, "ctx", split_axis=0, concat_axis=0, tiled=True),
    )
    heads = pieces[1].shape[2]
    query_own = settle(pieces[0], recv_place).reshape(length, heads, GROUP, HD)
    keys_own = settle(pieces[1], recv_place)
    values_own = settle(pieces[2], recv_place)
    grads_own = settle(pieces[3], recv_place).reshape(length, heads, GROUP, HD)
    before = from_behind(jnp.stack([keys_own, values_own]), "ctx", 1)
    results = block_attention(
        query_own, keys_own, values_own, grads_own, before[0], before[1], linked
    )
    attended, grad_q, key_own, key_prior, value_own, value_prior = results
    after = from_behind(jnp.stack([key_prior, value_prior]), "ctx", -1)
    grad_k = (key_own.astype(jnp.float32) + after[0].astype(jnp.float32)).astype(jnp.bfloat16)
    grad_v = (value_own.astype(jnp.float32) + after[1].astype(jnp.float32)).astype(jnp.bfloat16)
    back = (
        lax.all_to_all(
            returning(attended, back_order, heads, wide),
            "ctx",
            split_axis=0,
            concat_axis=0,
            tiled=True,
        ),
        lax.all_to_all(
            returning(grad_q, back_order, heads, wide),
            "ctx",
            split_axis=0,
            concat_axis=0,
            tiled=True,
        ),
        lax.all_to_all(
            returning(grad_k, back_order, heads, HD), "ctx", split_axis=0, concat_axis=0, tiled=True
        ),
        lax.all_to_all(
            returning(grad_v, back_order, heads, HD), "ctx", split_axis=0, concat_axis=0, tiled=True
        ),
    )
    outputs = tuple((settle(buffer, send_place) for buffer in back))
    attended = outputs[0].reshape(length, kv_heads * wide)
    grad_query = outputs[1].reshape(length, kv_heads * wide)
    grad_key = outputs[2].reshape(length, kv_heads * HD)
    grad_value = outputs[3].reshape(length, kv_heads * HD)
    partial_value = jnp.concatenate(
        [
            jnp.sum(grad_query.astype(jnp.float32), axis=0),
            jnp.sum(grad_value.astype(jnp.float32), axis=0),
        ]
    )
    share = sent_and_summed(partial_value, "ctx", 0)
    share = taken_together(share, "dp")
    summed = collect(share, "ctx", 0)
    bias_grad = summed * (1.0 / math.sqrt(length * devices * replicas))
    return (attended, grad_query, grad_key, grad_value, bias_grad)


def solution(mesh):
    in_specs = (
        P(("dp", "ctx"), None),
        P(("dp", "ctx"), None),
        P(("dp", "ctx"), None),
        P(("dp", "ctx"), None),
        P("dp", None),
        P("dp", "ctx"),
    )
    out_specs = (
        P(("dp", "ctx"), None),
        P(("dp", "ctx"), None),
        P(("dp", "ctx"), None),
        P(("dp", "ctx"), None),
        P(),
    )
    return jax.shard_map(local, mesh=mesh, in_specs=in_specs, out_specs=out_specs, check_vma=False)
```

profile of v0, /device:TPU:1, one launch (start us, length us, event | category | flops | bytes accessed | tf_op | source)
XLA Modules:
  0.0 464.3 jit_solution(16417272204320766600)
XLA Ops:
  1.6 3.3 fusion.3
  6.2 2.1 gather_fusion.1
  10.4 17.2 %all-to-all-start = ((bf16[32,8,4,128]{3,1,2,0:T(8,128)(2,1)}), bf16[32,8,4,128]{3,1,2,0:T(8,128)(2,1)S(1)}, u32[]{:S(2)}, u32[]{:S(2)}) async-start(bf16[32,8,4,128]{3,1,2,0:T(8,128)(2,1)} %get-tuple-element.40), calls=%async_computation | async-start | bytes 524288 | tf_op jit(solution)/shard_map/all_to_all | solution.py:149
  27.7 3.2 gather_fusion.5
  30.9 3.2 gather_fusion.9
  34.0 7.0 %all-to-all-done = bf16[32,8,4,128]{3,1,2,0:T(8,128)(2,1)S(1)} async-done(((bf16[32,8,4,128]{3,1,2,0:T(8,128)(2,1)}), bf16[32,8,4,128]{3,1,2,0:T(8,128)(2,1)S(1)}, u32[]{:S(2)}, u32[]{:S(2)}) %all-to-all-start) | async-done | bytes 262176 | tf_op jit(solution)/shard_map/all_to_all | solution.py:149
  41.0 6.0 %all-to-all-start.1 = ((bf16[32,8,4,128]{3,1,2,0:T(8,128)(2,1)}), bf16[32,8,4,128]{3,1,2,0:T(8,128)(2,1)S(1)}, u32[]{:S(2)}, u32[]{:S(2)}) async-start(bf16[32,8,4,128]{3,1,2,0:T(8,128)(2,1)} %get-tuple-element.39), calls=%async_computation.1 | async-start | bytes 524288 | tf_op jit(solution)/shard_map/all_to_all | solution.py:148
  47.1 3.9 broadcast_select_fusion.2
  51.0 9.5 %all-to-all-done.1 = bf16[32,8,4,128]{3,1,2,0:T(8,128)(2,1)S(1)} async-done(((bf16[32,8,4,128]{3,1,2,0:T(8,128)(2,1)}), bf16[32,8,4,128]{3,1,2,0:T(8,128)(2,1)S(1)}, u32[]{:S(2)}, u32[]{:S(2)}) %all-to-all-start.1) | async-done | bytes 262176 | tf_op jit(solution)/shard_map/all_to_all | solution.py:148
  60.5 55.8 %all_to_all.61 = bf16[32,8,4,1024]{3,1,2,0:T(8,128)(2,1)} all-to-all(bf16[32,8,4,1024]{3,1,2,0:T(8,128)(2,1)S(1)} %bitcast.226), channel_id=1, replica_groups=mesh['dp'=16,'ctx'=32] {'ctx'}, dimensions={0} | all-to-all | bytes 4194304 | tf_op jit(solution)/shard_map/all_to_all | solution.py:147
  116.3 9.2 %all-to-all-start.4 = ((bf16[32,8,4,1024]{3,1,2,0:T(8,128)(2,1)}), bf16[32,8,4,1024]{3,1,2,0:T(8,128)(2,1)S(1)}, u32[]{:S(2)}, u32[]{:S(2)}) async-start(bf16[32,8,4,1024]{3,1,2,0:T(8,128)(2,1)} %bitcast.224), calls=%async_computation.4 | async-start | bytes 4194304 | tf_op jit(solution)/shard_map/all_to_all | solution.py:150
  126.3 16.0 %scatter_custom_fusion.1 = s32[4096]{0:T(1024)S(1)} fusion(s32[4096]{0:T(1024)S(1)} %bitcast.245, s32[4096]{0:T(1024)S(1)} %iota.20, s32[]{:T(128)} %constant.81.clone.1), kind=kCustom, calls=%fused_computation.129 | custom fusion | bytes 16388 | tf_op jit(solution)/shard_map/scatter | solution.py:114
  147.5 3.5 collective-permute-start
  151.1 1.8 copy.355
  152.9 3.0 copy.231
  155.9 3.0 gather_fusion.6
  158.9 17.4 %all-to-all-done.4 = bf16[32,8,4,1024]{3,1,2,0:T(8,128)(2,1)S(1)} async-done(((bf16[32,8,4,1024]{3,1,2,0:T(8,128)(2,1)}), bf16[32,8,4,1024]{3,1,2,0:T(8,128)(2,1)S(1)}, u32[]{:S(2)}, u32[]{:S(2)}) %all-to-all-start.4) | async-done | bytes 2097184 | tf_op jit(solution)/shard_map/all_to_all | solution.py:150
  176.5 1.6 copy.244
  178.1 2.4 gather_fusion.10
  180.5 2.2 broadcast_select_fusion.6
  182.7 1.4 reshape.257
  186.6 1.6 bitcast_reduce_fusion
  189.1 2.3 fusion.4
  191.4 2.5 fusion.7
  193.9 1.7 copy.264
  195.6 1.9 fusion.38
  197.4 1.7 copy.256
  199.2 1.9 fusion.40
  201.1 1.7 copy.258
  202.7 1.7 fusion.25
  204.4 1.7 copy.257
  206.1 2.2 fusion.26
  208.3 2.1 collective-permute-start.1
  211.6 2.4 add_convert_fusion.1
  214.0 2.1 copy.238
  216.0 3.1 add_convert_fusion
  219.2 1.9 copy.251
  221.0 3.6 gather_fusion.7
  224.6 3.6 gather_fusion.11
  228.2 1.6 fusion.35
  233.8 12.6 %all-to-all-start.7 = ((bf16[32,8,4,128]{3,1,2,0:T(8,128)(2,1)}), bf16[32,8,4,128]{3,1,2,0:T(8,128)(2,1)S(1)}, u32[]{:S(2)}, u32[]{:S(2)}) async-start(bf16[32,8,4,128]{3,1,2,0:T(8,128)(2,1)} %copy.267), calls=%async_computation.7 | async-start | bytes 524288 | tf_op jit(solution)/shard_map/all_to_all | solution.py:183
  246.4 4.6 broadcast_select_fusion
  251.0 2.2 copy.253
  253.2 6.4 %all-to-all-done.7 = bf16[32,8,4,128]{3,1,2,0:T(8,128)(2,1)S(1)} async-done(((bf16[32,8,4,128]{3,1,2,0:T(8,128)(2,1)}), bf16[32,8,4,128]{3,1,2,0:T(8,128)(2,1)S(1)}, u32[]{:S(2)}, u32[]{:S(2)}) %all-to-all-start.7) | async-done | bytes 262176 | tf_op jit(solution)/shard_map/all_to_all | solution.py:183
  259.6 6.2 %all-to-all-start.5 = ((bf16[32,8,4,1024]{3,1,2,0:T(8,128)(2,1)}), bf16[32,8,4,1024]{3,1,2,0:T(8,128)(2,1)S(1)}, u32[]{:S(2)}, u32[]{:S(2)}) async-start(bf16[32,8,4,1024]{3,1,2,0:T(8,128)(2,1)} %copy.253), calls=%async_computation.5 | async-start | bytes 4194304 | tf_op jit(solution)/shard_map/all_to_all | solution.py:173
  267.6 49.2 %all-to-all-done.5 = bf16[32,8,4,1024]{3,1,2,0:T(8,128)(2,1)S(1)} async-done(((bf16[32,8,4,1024]{3,1,2,0:T(8,128)(2,1)}), bf16[32,8,4,1024]{3,1,2,0:T(8,128)(2,1)S(1)}, u32[]{:S(2)}, u32[]{:S(2)}) %all-to-all-start.5) | async-done | bytes 2097184 | tf_op jit(solution)/shard_map/all_to_all | solution.py:173
  316.8 12.7 %all-to-all-start.6 = ((bf16[32,8,4,128]{3,1,2,0:T(8,128)(2,1)}), bf16[32,8,4,128]{3,1,2,0:T(8,128)(2,1)S(1)}, u32[]{:S(2)}, u32[]{:S(2)}) async-start(bf16[32,8,4,128]{3,1,2,0:T(8,128)(2,1)} %copy.261), calls=%async_computation.6 | async-start | bytes 524288 | tf_op jit(solution)/shard_map/all_to_all | solution.py:180
  330.0 2.9 copy.255
  332.9 3.2 gather_fusion.12
  336.1 1.7 convert_reduce_fusion
  338.6 4.0 all-to-all-done.6
  342.6 8.2 %all-to-all-start.8 = ((f32[32,1,144]{2,1,0:T(1,128)}), f32[32,1,144]{2,1,0:T(1,128)S(1)}, u32[]{:S(2)}, u32[]{:S(2)}) async-start(f32[32,1,144]{2,1,0:T(1,128)} %all_to_all.46), calls=%async_computation.8 | async-start | bytes 65536 | tf_op jit(solution)/shard_map/all_to_all | solution.py:25
  350.8 2.2 copy.240
  353.1 9.6 %all-to-all-done.8 = f32[32,1,144]{2,1,0:T(1,128)S(1)} async-done(((f32[32,1,144]{2,1,0:T(1,128)}), f32[32,1,144]{2,1,0:T(1,128)S(1)}, u32[]{:S(2)}, u32[]{:S(2)}) %all-to-all-start.8) | async-done | bytes 18464 | tf_op jit(solution)/shard_map/all_to_all | solution.py:25
  362.6 4.5 all-to-all-start.3
  368.4 49.7 %all-to-all-done.3 = bf16[32,8,4,1024]{3,1,2,0:T(8,128)(2,1)S(1)} async-done(((bf16[32,8,4,1024]{3,1,2,0:T(8,128)(2,1)}), bf16[32,8,4,1024]{3,1,2,0:T(8,128)(2,1)S(1)}, u32[]{:S(2)}, u32[]{:S(2)}) %all-to-all-start.3) | async-done | bytes 2097184 | tf_op jit(solution)/shard_map/all_to_all | solution.py:166
  418.7 15.0 %all-to-all-start.9 = ((f32[16,1,144]{2,1,0:T(1,128)}), f32[16,1,144]{2,1,0:T(1,128)S(1)}, u32[]{:S(2)}, u32[]{:S(2)}) async-start(f32[16,1,144]{2,1,0:T(1,128)} %broadcast_in_dim.102), calls=%async_computation.9 | async-start | bytes 32768 | tf_op jit(solution)/shard_map/all_to_all | solution.py:31
  434.6 1.6 copy.242
  436.2 1.4 gather_fusion.8
  437.7 2.8 all-to-all-done.9
  441.2 10.1 %all-to-all-start.10 = ((f32[32,1,144]{2,1,0:T(1,128)}), f32[32,1,144]{2,1,0:T(1,128)S(1)}, u32[]{:S(2)}, u32[]{:S(2)}) async-start(f32[32,1,144]{2,1,0:T(1,128)} %broadcast_in_dim.103), calls=%async_computation.10 | async-start | bytes 65536 | tf_op jit(solution)/shard_map/all_to_all | solution.py:31
  451.8 1.3 copy.303
  453.2 1.3 copy.302
  454.5 8.5 %all-to-all-done.10 = f32[32,1,144]{2,1,0:T(1,128)S(1)} async-done(((f32[32,1,144]{2,1,0:T(1,128)}), f32[32,1,144]{2,1,0:T(1,128)S(1)}, u32[]{:S(2)}, u32[]{:S(2)}) %all-to-all-start.10) | async-done | bytes 18464 | tf_op jit(solution)/shard_map/all_to_all | solution.py:31
  (108 shorter events, 26.0 us)
Async XLA Ops:
  0.6 27.0 %copy-start = (bf16[128,4096]{1,0:T(8,128)(2,1)S(1)}, bf16[128,4096]{1,0:T(8,128)(2,1)}, u32[]{:S(2)}) copy-start(bf16[128,4096]{1,0:T(8,128)(2,1)} %param.18) | copy-start | bytes 3145732
  0.6 7.7 %copy-start.3 = (bf16[128,512]{1,0:T(8,128)(2,1)S(1)}, bf16[128,512]{1,0:T(8,128)(2,1)}, u32[]{:S(2)}) copy-start(bf16[128,512]{1,0:T(8,128)(2,1)} %param.19) | copy-start | bytes 393220
  10.4 30.6 %all-to-all-start = ((bf16[32,8,4,128]{3,1,2,0:T(8,128)(2,1)}), bf16[32,8,4,128]{3,1,2,0:T(8,128)(2,1)S(1)}, u32[]{:S(2)}, u32[]{:S(2)}) async-start(bf16[32,8,4,128]{3,1,2,0:T(8,128)(2,1)} %get-tuple-element.40), calls=%async_computation | async-start | bytes 524288 | tf_op jit(solution)/shard_map/all_to_all | solution.py:149
  27.6 3.2 copy-start.2
  41.0 19.4 %all-to-all-start.1 = ((bf16[32,8,4,128]{3,1,2,0:T(8,128)(2,1)}), bf16[32,8,4,128]{3,1,2,0:T(8,128)(2,1)S(1)}, u32[]{:S(2)}, u32[]{:S(2)}) async-start(bf16[32,8,4,128]{3,1,2,0:T(8,128)(2,1)} %get-tuple-element.39), calls=%async_computation.1 | async-start | bytes 524288 | tf_op jit(solution)/shard_map/all_to_all | solution.py:148
  116.3 9.9 %copy-start.15 = (s32[1,4096]{1,0:T(1,128)S(1)}, s32[1,4096]{1,0:T(1,128)}, u32[]{:S(2)}) copy-start(s32[1,4096]{1,0:T(1,128)} %param.22) | copy-start | bytes 49156
  116.3 60.0 %all-to-all-start.4 = ((bf16[32,8,4,1024]{3,1,2,0:T(8,128)(2,1)}), bf16[32,8,4,1024]{3,1,2,0:T(8,128)(2,1)S(1)}, u32[]{:S(2)}, u32[]{:S(2)}) async-start(bf16[32,8,4,1024]{3,1,2,0:T(8,128)(2,1)} %bitcast.224), calls=%async_computation.4 | async-start | bytes 4194304 | tf_op jit(solution)/shard_map/all_to_all | solution.py:150
  147.5 39.0 %collective-permute-start = (bf16[2,128,4,128]{3,1,2,0:T(8,128)(2,1)}, bf16[2,128,4,128]{3,1,2,0:T(8,128)(2,1)}, u32[]{:S(2)}, u32[]{:S(2)}) collective-permute-start(bf16[2,128,4,128]{3,1,2,0:T(8,128)(2,1)} %pad_maximum_fusion), channel_id=1, source_target_pairs={{0,1},{1,2},{2,3},{3,4},{4,5},{5,6},{6,7},{7,8},{8,9},{9,10},{10,1... | collective-permute-start | bytes 786440 | tf_op jit(solution)/shard_map/ppermute | solution.py:15
  184.1 1.2 copy-start.11
  185.3 3.7 copy-start.9
  199.2 1.9 copy-start.4
  201.1 1.7 copy-start.10
  206.1 4.3 copy-start.12
  206.1 4.3 copy-start.14
  208.3 3.3 copy-start.6
  208.3 19.9 %collective-permute-start.1 = (bf16[2,128,4,128]{1,3,2,0:T(8,128)(2,1)S(1)}, bf16[2,128,4,128]{1,3,2,0:T(8,128)(2,1)}, u32[]{:S(2)}, u32[]{:S(2)}) collective-permute-start(bf16[2,128,4,128]{1,3,2,0:T(8,128)(2,1)S(1)} %pad_maximum_fusion.1), channel_id=1, source_target_pairs={{1,0},{2,1},{3,2},{4,3},{5,4},{6,5},{7,6},{8,7},{9,8},{10,9},{11,1... | collective-permute-start | bytes 786440 | tf_op jit(solution)/shard_map/ppermute | solution.py:15
  224.6 3.6 copy-start.13
  229.8 16.6 %copy-start.5 = (bf16[256,4,1024]{2,1,0:T(4,128)(2,1)S(1)}, bf16[256,4,1024]{2,1,0:T(4,128)(2,1)}, u32[]{:S(2)}) copy-start(bf16[256,4,1024]{2,1,0:T(4,128)(2,1)} %gather_fusion.7) | copy-start | bytes 6291460
  233.8 25.8 %all-to-all-start.7 = ((bf16[32,8,4,128]{3,1,2,0:T(8,128)(2,1)}), bf16[32,8,4,128]{3,1,2,0:T(8,128)(2,1)S(1)}, u32[]{:S(2)}, u32[]{:S(2)}) async-start(bf16[32,8,4,128]{3,1,2,0:T(8,128)(2,1)} %copy.267), calls=%async_computation.7 | async-start | bytes 524288 | tf_op jit(solution)/shard_map/all_to_all | solution.py:183
  259.6 57.3 %all-to-all-start.5 = ((bf16[32,8,4,1024]{3,1,2,0:T(8,128)(2,1)}), bf16[32,8,4,1024]{3,1,2,0:T(8,128)(2,1)S(1)}, u32[]{:S(2)}, u32[]{:S(2)}) async-start(bf16[32,8,4,1024]{3,1,2,0:T(8,128)(2,1)} %copy.253), calls=%async_computation.5 | async-start | bytes 4194304 | tf_op jit(solution)/shard_map/all_to_all | solution.py:173
  316.8 25.8 %all-to-all-start.6 = ((bf16[32,8,4,128]{3,1,2,0:T(8,128)(2,1)}), bf16[32,8,4,128]{3,1,2,0:T(8,128)(2,1)S(1)}, u32[]{:S(2)}, u32[]{:S(2)}) async-start(bf16[32,8,4,128]{3,1,2,0:T(8,128)(2,1)} %copy.261), calls=%async_computation.6 | async-start | bytes 524288 | tf_op jit(solution)/shard_map/all_to_all | solution.py:180
  332.9 17.9 %copy-start.7 = (bf16[256,4,1024]{2,1,0:T(4,128)(2,1)S(1)}, bf16[256,4,1024]{2,1,0:T(4,128)(2,1)}, u32[]{:S(2)}) copy-start(bf16[256,4,1024]{2,1,0:T(4,128)(2,1)} %get-tuple-element.32) | copy-start | bytes 6291460
  342.6 20.0 %all-to-all-start.8 = ((f32[32,1,144]{2,1,0:T(1,128)}), f32[32,1,144]{2,1,0:T(1,128)S(1)}, u32[]{:S(2)}, u32[]{:S(2)}) async-start(f32[32,1,144]{2,1,0:T(1,128)} %all_to_all.46), calls=%async_computation.8 | async-start | bytes 65536 | tf_op jit(solution)/shard_map/all_to_all | solution.py:25
  362.6 55.4 %all-to-all-start.3 = ((bf16[32,8,4,1024]{3,1,2,0:T(8,128)(2,1)}), bf16[32,8,4,1024]{3,1,2,0:T(8,128)(2,1)S(1)}, u32[]{:S(2)}, u32[]{:S(2)}) async-start(bf16[32,8,4,1024]{3,1,2,0:T(8,128)(2,1)} %copy.240), calls=%async_computation.3 | async-start | bytes 4194304 | tf_op jit(solution)/shard_map/all_to_all | solution.py:166
  418.7 21.8 %all-to-all-start.9 = ((f32[16,1,144]{2,1,0:T(1,128)}), f32[16,1,144]{2,1,0:T(1,128)S(1)}, u32[]{:S(2)}, u32[]{:S(2)}) async-start(f32[16,1,144]{2,1,0:T(1,128)} %broadcast_in_dim.102), calls=%async_computation.9 | async-start | bytes 32768 | tf_op jit(solution)/shard_map/all_to_all | solution.py:31
  437.7 14.1 %copy-start.8 = (bf16[128,4,1024]{2,1,0:T(4,128)(2,1)S(1)}, bf16[128,4,1024]{2,1,0:T(4,128)(2,1)}, u32[]{:S(2)}) copy-start(bf16[128,4,1024]{2,1,0:T(4,128)(2,1)} %get-tuple-element.16) | copy-start | bytes 3145732
  441.2 21.8 %all-to-all-start.10 = ((f32[32,1,144]{2,1,0:T(1,128)}), f32[32,1,144]{2,1,0:T(1,128)S(1)}, u32[]{:S(2)}, u32[]{:S(2)}) async-start(f32[32,1,144]{2,1,0:T(1,128)} %broadcast_in_dim.103), calls=%async_computation.10 | async-start | bytes 65536 | tf_op jit(solution)/shard_map/all_to_all | solution.py:31
  451.8 12.0 %copy-start.1 = (bf16[128,4096]{1,0:T(8,128)(2,1)S(1)}, bf16[128,4096]{1,0:T(8,128)(2,1)}, u32[]{:S(2)}) copy-start(bf16[128,4096]{1,0:T(8,128)(2,1)} %param.18) | copy-start | bytes 3145732
where the time goes:
time: 473 us; the launch traced here: 464 us
  waiting for transfers between devices  164 us (35%)
  starting transfers between devices  107 us (23%)
  local copies, waits for them, and re-layouts  90.1 us (19%)
  blocking collectives  55.8 us (12%)
  other arithmetic  23.5 us (5%)
  matrix products  21 us (4%)
    all_to_all x1, blocking collectives, local(): lax.all_to_all(queries, 'ctx', split_axis=0, concat_axis=0, tiled=True)  55.8 us
    all_to_all x1, waiting for transfers between devices, local(): lax.all_to_all(returning(attended, back_order, heads, wide), 'ctx', split...  49.7 us
    all_to_all x1, waiting for transfers between devices, local(): lax.all_to_all(returning(grad_q, back_order, heads, wide), 'ctx', split_a...  49.2 us
    all_to_all x2, starting transfers between devices, from_everyone(): lax.all_to_all(jnp.broadcast_to(shard[None], (count, *shard.shape)), axis...  25 us
    dot_general x12, matrix products, product(): return jnp.einsum(form, left, right, preferred_element_type=jnp.float32)  21 us
    all_to_all x1, waiting for transfers between devices, local(): lax.all_to_all(grads_out, 'ctx', split_axis=0, concat_axis=0, tiled=True)  17.4 us
    all_to_all x1, starting transfers between devices, local(): lax.all_to_all(values_out, 'ctx', split_axis=0, concat_axis=0, tiled=True)  17.2 us
    scatter x1, local copies, waits for them, and re-layouts, local(): jnp.zeros_like(plan).at[plan]  16 us
  transfers between devices with their start and end apart: 12, of which 10 were waited for; matrix products, arithmetic and copies ran while one was open for 20% of the time, Pallas kernels for 0%

commit v1 on v0

v1 whole, which is shorter than its diff:
```python
import functools

import jax
import jax.numpy as jnp
from jax import lax
from jax.experimental import pallas as pl
from jax.experimental.pallas import tpu as pltpu
from jax.sharding import PartitionSpec as P

MESH = pl.DeviceIdType.MESH
VMEM = pl.BlockSpec(memory_space=pltpu.VMEM)
ANY = pl.BlockSpec(memory_space=pl.ANY)
F32 = jnp.float32
BF16 = jnp.bfloat16


def places():
    dp = lax.axis_index("dp")
    ctx = lax.axis_index("ctx")
    return dp, ctx, ctx // 16, lax.rem(ctx // 2, 8), lax.rem(ctx, 2)


def at_ctx(dp, yh, z, c):
    return (dp, yh * 16 + z * 2 + c)


def cols(start, size):
    return pl.ds(pl.multiple_of(start, 128), size)


def gather_kernel(q, k, v, g, lk, KV, QX, GX, LK, local_sem, core_send, core_recv,
                  y_send, y_recv, z_send, z_recv, l_send, l_recv):
    dp, ctx, yh, z, c = places()
    mine, other = pl.ds(c * 128, 128), 1 - c
    half = pl.ds(0, 128), pl.ds(128, 128)

    def local_pair(i, src, dst):
        copy = pltpu.make_async_copy(src, dst, local_sem.at[i])
        copy.start()
        return copy

    local = []
    for gi in range(2):
        local.append(local_pair(2 * gi, k.at[:, cols((2 * c + gi) * 128, 128)], KV.at[gi, yh, z, mine, half[0]]))
        local.append(local_pair(2 * gi + 1, v.at[:, cols((2 * c + gi) * 128, 128)], KV.at[gi, yh, z, mine, half[1]]))
    local.append(local_pair(4, q.at[:, cols(c * 2048, 2048)], QX.at[mine, :]))
    local.append(local_pair(5, g.at[:, cols(c * 2048, 2048)], GX.at[mine, :]))
    LK[ctx] = lk[0]

    barrier = pltpu.get_barrier_semaphore()
    for i in range(1, 32):
        pl.semaphore_signal(barrier, inc=1, device_id=(dp, lax.rem(ctx + i, 32)), device_id_type=MESH)
    pl.semaphore_wait(barrier, 31)

    def remote(src, dst, send, recv, device):
        copy = pltpu.make_async_remote_copy(src_ref=src, dst_ref=dst, send_sem=send, recv_sem=recv,
                                            device_id=device, device_id_type=MESH)
        copy.start()
        return copy

    pending = []
    partner = at_ctx(dp, yh, z, other)
    core = []
    for gi in range(2):
        for j, src in ((0, k), (1, v)):
            i = 2 * gi + j
            core.append(remote(src.at[:, cols((2 * other + gi) * 128, 128)], KV.at[gi, yh, z, mine, half[j]],
                               core_send.at[i], core_recv.at[i], partner))
    for i, (src, dst) in ((4, (q, QX)), (5, (g, GX))):
        core.append(remote(src.at[:, cols(other * 2048, 2048)], dst.at[mine, :],
                           core_send.at[i], core_recv.at[i], partner))

    right = at_ctx(dp, yh, lax.rem(z + 1, 8), c)
    left = at_ctx(dp, yh, lax.rem(z + 7, 8), c)
    rows = {}

    def chunk(gi, far, zz, part):
        y = 1 - yh if far else yh
        ref = KV.at[gi, y, lax.rem(zz + 8, 8)]
        return ref if part is None else ref.at[half[part], :]

    def step(gi, far, s):
        item = 2 * far + gi
        for way in range(2):
            if s > 0:
                rows[(item, way, s - 1)].wait_recv()
            part = way if s == 3 else None
            ref = chunk(gi, far, z - s if way == 0 else z + s, part)
            copy = remote(ref, ref, z_send.at[item, way, s], z_recv.at[item, way, s], right if way == 0 else left)
            rows[(item, way, s)] = copy
            pending.append(copy)

    ys = []
    for gi in range(2):
        for i in (2 * gi, 2 * gi + 1):
            local[i].wait()
            core[i].wait_recv()
        step(gi, 0, 0)
        ref = KV.at[gi, yh, z]
        ys.append(remote(ref, ref, y_send.at[gi], y_recv.at[gi], at_ctx(dp, 1 - yh, z, c)))
    flags = []
    for i in range(1, 32):
        flags.append(remote(lk.at[0], LK.at[ctx], l_send.at[i - 1], l_recv.at[i - 1], (dp, lax.rem(ctx + i, 32))))
    for s in (1,):
        step(0, 0, s)
        step(1, 0, s)
    for gi in range(2):
        ys[gi].wait_recv()
        step(gi, 1, 0)
    for s in (1, 2):
        step(0, 0, s + 1)
        step(1, 0, s + 1)
        step(0, 1, s)
        step(1, 1, s)
    step(0, 1, 3)
    step(1, 1, 3)
    for item in range(4):
        for way in range(2):
            rows[(item, way, 3)].wait_recv()
    for copy in pending + ys + core:
        copy.wait_send()
    local[4].wait()
    local[5].wait()
    core[4].wait_recv()
    core[5].wait_recv()
    for copy in flags:
        copy.wait()


def gathered(q, k, v, g, lk):
    return pl.pallas_call(
        gather_kernel,
        out_shape=(
            jax.ShapeDtypeStruct((2, 2, 8, 256, 256), BF16),
            jax.ShapeDtypeStruct((256, 2048), BF16),
            jax.ShapeDtypeStruct((256, 2048), BF16),
            jax.ShapeDtypeStruct((32, 1, 128), jnp.int32),
        ),
        in_specs=[ANY, ANY, ANY, ANY, VMEM],
        out_specs=(VMEM, VMEM, VMEM, VMEM),
        scratch_shapes=[
            pltpu.SemaphoreType.DMA((6,)),
            pltpu.SemaphoreType.DMA((6,)),
            pltpu.SemaphoreType.DMA((6,)),
            pltpu.SemaphoreType.DMA((2,)),
            pltpu.SemaphoreType.DMA((2,)),
            pltpu.SemaphoreType.DMA((4, 2, 4)),
            pltpu.SemaphoreType.DMA((4, 2, 4)),
            pltpu.SemaphoreType.DMA((31,)),
            pltpu.SemaphoreType.DMA((31,)),
        ],
        compiler_params=pltpu.CompilerParams(collective_id=0, has_side_effects=True, vmem_limit_bytes=48 * 2**20),
        name="gather",
    )(q, k, v, g, lk)


def dot(a, b, ca, cb):
    return lax.dot_general(a, b, (((ca,), (cb,)), ((), ())), preferred_element_type=F32)


def attention_kernel(own, KV, QX, GX, LK, PR, PP, PQ, D, ATT, GQ, BV, QP, GP, OP, DQP, PAD, SLOT, DS):
    chip = own[0]
    scale = 128**-0.5

    def placing(c):
        return (PR[c] == lax.broadcasted_iota(jnp.int32, (512, 256), 0)).astype(BF16)

    mine = placing(chip)

    def spread(j, _):
        at = cols(j * 256, 256)
        QP[:, at] = dot(mine, QX[:, at], 1, 0).astype(BF16)
        GP[:, at] = dot(mine, GX[:, at], 1, 0).astype(BF16)
        return 0

    lax.fori_loop(0, 8, spread, 0)
    BV[...] = jnp.zeros_like(BV)
    SLOT[0] = jnp.zeros((128, 256), BF16)

    for gi in range(2):
        def widen(c, _):
            found = dot(placing(c), KV[gi, c // 8, lax.rem(c, 8)], 1, 0).astype(BF16)
            PAD[:, pl.ds(pl.multiple_of(c * 16, 16), 16), :] = found.reshape(32, 16, 256)
            return 0

        lax.fori_loop(0, 16, widen, 0)

        def seat(b):
            return (PP[b] == lax.broadcasted_iota(jnp.int32, (128, 256), 0) + 1).astype(BF16)

        def settle(b, _):
            SLOT[b + 1] = dot(seat(b), PAD[b], 1, 0).astype(BF16)
            return 0

        lax.fori_loop(0, 32, settle, 0)
        DS[0] = jnp.zeros((128, 256), F32)

        def block(b, _):
            keys = jnp.concatenate([SLOT[b, :, 0:128], SLOT[b + 1, :, 0:128]], axis=0)
            values = jnp.concatenate([SLOT[b, :, 128:256], SLOT[b + 1, :, 128:256]], axis=0)
            at = pl.ds(pl.multiple_of(b * 16, 16), 16)
            q = jnp.concatenate([QP[at, (gi * 8 + h) * 128:(gi * 8 + h + 1) * 128] for h in range(8)], axis=0)
            o = jnp.concatenate([GP[at, (gi * 8 + h) * 128:(gi * 8 + h + 1) * 128] for h in range(8)], axis=0)
            u = lax.broadcasted_iota(jnp.int32, (128, 128), 0)
            seen_own = u <= PQ[b]
            seen_prior = jnp.broadcast_to(LK[b] > 0, (128, 128))
            seen = jnp.concatenate([seen_prior, seen_own], axis=0)
            s = jnp.where(seen, dot(keys, q, 1, 1), -jnp.inf)
            top = jnp.max(s, axis=0, keepdims=True)
            e = jnp.exp((s - top) * scale)
            probs = e * (1.0 / jnp.sum(e, axis=0, keepdims=True))
            press = dot(values, o, 1, 1)
            both = probs * press
            centred = jnp.sum(both, axis=0, keepdims=True)
            slopes = ((both - probs * centred) * scale).astype(BF16)
            weights = probs.astype(BF16)
            att = dot(weights, values, 0, 0).astype(BF16)
            gq = dot(slopes, keys, 0, 0).astype(BF16)
            for h in range(8):
                to = slice((gi * 8 + h) * 128, (gi * 8 + h + 1) * 128)
                OP[at, to] = att[h * 16:(h + 1) * 16]
                DQP[at, to] = gq[h * 16:(h + 1) * 16]
            dk = dot(slopes, q, 1, 0)
            dv = dot(weights, o, 1, 0)
            DS[b, :, 0:128] += dk[0:128]
            DS[b, :, 128:256] += dv[0:128]
            DS[b + 1, :, 0:128] = dk[128:256]
            DS[b + 1, :, 128:256] = dv[128:256]
            return 0

        lax.fori_loop(0, 32, block, 0)

        def unseat(b, total):
            grads = DS[b + 1]
            PAD[b] = dot(seat(b), grads.astype(BF16), 0, 0).astype(BF16)
            return total + jnp.sum(grads[:, 128:256].reshape(16, 8, 128), axis=0)

        total = lax.fori_loop(0, 32, unseat, jnp.zeros((8, 128), F32))
        BV[16 + gi:17 + gi, :] = jnp.sum(total, axis=0, keepdims=True)

        def narrow(c, _):
            rows = PAD[:, pl.ds(pl.multiple_of(c * 16, 16), 16), :].reshape(512, 256)
            D[gi, c // 8, lax.rem(c, 8)] = dot(placing(c), rows, 0, 0).astype(BF16)
            return 0

        lax.fori_loop(0, 16, narrow, 0)

    for j in range(8):
        at = slice(j * 256, (j + 1) * 256)
        ATT[:, at] = dot(mine, OP[:, at], 0, 0).astype(BF16)
        rows = dot(mine, DQP[:, at], 0, 0)
        GQ[:, at] = rows.astype(BF16)
        sums = jnp.sum(rows, axis=0, keepdims=True)
        BV[2 * j:2 * j + 1, :] = sums[:, 0:128]
        BV[2 * j + 1:2 * j + 2, :] = sums[:, 128:256]


def attended(own, KV, QX, GX, LK, PR, PP, PQ):
    return pl.pallas_call(
        attention_kernel,
        out_shape=(
            jax.ShapeDtypeStruct((2, 2, 8, 256, 256), BF16),
            jax.ShapeDtypeStruct((256, 2048), BF16),
            jax.ShapeDtypeStruct((256, 2048), BF16),
            jax.ShapeDtypeStruct((24, 128), F32),
        ),
        in_specs=[pl.BlockSpec(memory_space=pltpu.SMEM)] + [VMEM] * 7,
        out_specs=(VMEM,) * 4,
        scratch_shapes=[
            pltpu.VMEM((512, 2048), BF16),
            pltpu.VMEM((512, 2048), BF16),
            pltpu.VMEM((512, 2048), BF16),
            pltpu.VMEM((512, 2048), BF16),
            pltpu.VMEM((32, 256, 256), BF16),
            pltpu.VMEM((33, 128, 256), BF16),
            pltpu.VMEM((33, 128, 256), F32),
        ],
        compiler_params=pltpu.CompilerParams(vmem_limit_bytes=58 * 2**20),
        name="attend",
    )(own, KV, QX, GX, LK, PR, PP, PQ)


def reduce_kernel(D, ATT, GQ, BV, att, gq, gk, gv, BT, R, YS, YR, KS, KR, BZ, BY, BX, BM,
                  local_sem, core_send, core_recv, k_send, k_recv, y_send, y_recv, z_send, z_recv,
                  b_send, b_recv):
    dp, ctx, yh, z, c = places()
    yl, x = dp // 4, lax.rem(dp, 4)
    y = yh * 4 + yl
    other = 1 - c
    half = pl.ds(0, 128), pl.ds(128, 128)

    def at_y(yy):
        return ((lax.rem(yy, 4)) * 4 + x, (yy // 4) * 16 + z * 2 + c)

    partner = at_ctx(dp, yh, z, other)
    along_z = [(lax.rem(z + i, 8), at_ctx(dp, yh, lax.rem(z + i, 8), c)) for i in range(1, 8)]
    along_y = [(lax.rem(y + i, 8), at_y(lax.rem(y + i, 8))) for i in range(1, 8)]
    along_x = [(lax.rem(x + i, 4), (yl * 4 + lax.rem(x + i, 4), ctx)) for i in range(1, 4)]
    barrier = pltpu.get_barrier_semaphore()
    for _, device in along_z + along_y + along_x + [(0, partner)]:
        pl.semaphore_signal(barrier, inc=1, device_id=device, device_id_type=MESH)
    pl.semaphore_wait(barrier, 18)

    def remote(src, dst, send, recv, device):
        copy = pltpu.make_async_remote_copy(src_ref=src, dst_ref=dst, send_sem=send, recv_sem=recv,
                                            device_id=device, device_id_type=MESH)
        copy.start()
        return copy

    sent = []
    rows = {}
    right, left = along_z[0][1], along_z[6][1]

    def side(far):
        return 1 - yh if far else yh

    def own(gi, far, zz):
        return D.at[gi, side(far), lax.rem(zz + 8, 8)]

    def step(gi, far, s):
        item = 2 * far + gi
        for way in range(2):
            device = right if way == 0 else left
            target = z + 4 - s if way == 0 else z - 4 + s
            dst = R.at[item, way, s]
            if s == 0:
                src = own(gi, far, target).at[half[way], :]
                dst = dst.at[half[way], :]
            else:
                rows[(item, way, s - 1)].wait_recv()
                src = R.at[item, way, s - 1]
                term = own(gi, far, target)
                for part in range(2):
                    at = slice(part * 128, part * 128 + 128)
                    if s == 1 and part != way:
                        src[at, :] = term[at, :]
                    else:
                        src[at, :] = (src[at, :].astype(F32) + term[at, :].astype(F32)).astype(BF16)
            copy = remote(src, dst, z_send.at[item, way, s], z_recv.at[item, way, s], device)
            rows[(item, way, s)] = copy
            sent.append(copy)

    def total(gi, far, at):
        item = 2 * far + gi
        return (D[gi, side(far), z, at, :].astype(F32) + R[item, 0, 3, at, :].astype(F32)
                + R[item, 1, 3, at, :].astype(F32))

    step(0, 1, 0)
    step(1, 1, 0)
    step(0, 0, 0)
    step(1, 0, 0)

    def spread(buffer, place, line, base, value):
        buffer[place] = value
        out = []
        for i, (_, device) in enumerate(line):
            out.append(remote(buffer.at[place], buffer.at[place], b_send.at[base + i], b_recv.at[base + i], device))
        return out

    def summed(buffer, copies, count):
        for copy in copies:
            copy.wait_recv()
        value = buffer[0]
        for i in range(1, count):
            value = value + buffer[i]
        return value

    copies_z = spread(BZ, z, along_z, 0, BV[...])
    local = []
    core = []
    for i, (src, dst) in enumerate(((ATT, att), (GQ, gq))):
        copy = pltpu.make_async_copy(src.at[pl.ds(c * 128, 128), :], dst.at[:, cols(c * 2048, 2048)], local_sem.at[i])
        copy.start()
        local.append(copy)
        core.append(remote(src.at[pl.ds(other * 128, 128), :], dst.at[:, cols(c * 2048, 2048)],
                           core_send.at[i], core_recv.at[i], partner))

    step(0, 1, 1)
    step(1, 1, 1)
    copies_y = spread(BY, y, along_y, 7, summed(BZ, copies_z, 8))
    step(0, 1, 2)
    step(1, 1, 2)
    step(0, 0, 1)
    step(1, 0, 1)
    copies_x = spread(BX, x, along_x, 14, summed(BY, copies_y, 8))
    step(0, 1, 3)
    step(1, 1, 3)
    step(0, 0, 2)
    step(1, 0, 2)
    BM[...] = summed(BX, copies_x, 4) * (65536.0**-0.5)
    BT[c] = BM[...]
    copies_m = [remote(BM, BT.at[c], b_send.at[17], b_recv.at[17], partner)]
    ys = []
    for gi in range(2):
        rows[(2 + gi, 0, 3)].wait_recv()
        rows[(2 + gi, 1, 3)].wait_recv()
        YS[gi] = total(gi, 1, slice(0, 256)).astype(BF16)
        ys.append(remote(YS.at[gi], YR.at[gi], y_send.at[gi], y_recv.at[gi], at_ctx(dp, 1 - yh, z, c)))
    step(0, 0, 3)
    step(1, 0, 3)
    ks = []
    for gi in range(2):
        rows[(gi, 0, 3)].wait_recv()
        rows[(gi, 1, 3)].wait_recv()
        ys[gi].wait_recv()
        at = pl.ds(pl.multiple_of(other * 128, 128), 128)
        KS[gi] = (total(gi, 0, at) + YR[gi, at, :].astype(F32)).astype(BF16)
        ks.append(remote(KS.at[gi], KR.at[gi], k_send.at[gi], k_recv.at[gi], partner))
        at = pl.ds(pl.multiple_of(c * 128, 128), 128)
        done = (total(gi, 0, at) + YR[gi, at, :].astype(F32)).astype(BF16)
        gk[:, cols((2 * c + gi) * 128, 128)] = done[:, 0:128]
        gv[:, cols((2 * c + gi) * 128, 128)] = done[:, 128:256]
    for gi in range(2):
        ks[gi].wait_recv()
        gk[:, cols((2 * other + gi) * 128, 128)] = KR[gi, :, 0:128]
        gv[:, cols((2 * other + gi) * 128, 128)] = KR[gi, :, 128:256]
    copies_m[0].wait_recv()
    for copy in sent + ys + ks + copies_z + copies_y + copies_x + copies_m + core:
        copy.wait_send()
    for copy in core:
        copy.wait_recv()
    for copy in local:
        copy.wait()


def reduced(D, ATT, GQ, BV):
    dma = pltpu.SemaphoreType.DMA
    return pl.pallas_call(
        reduce_kernel,
        out_shape=(
            jax.ShapeDtypeStruct((128, 4096), BF16),
            jax.ShapeDtypeStruct((128, 4096), BF16),
            jax.ShapeDtypeStruct((128, 512), BF16),
            jax.ShapeDtypeStruct((128, 512), BF16),
            jax.ShapeDtypeStruct((2, 24, 128), F32),
        ),
        in_specs=[VMEM] * 4,
        out_specs=(ANY, ANY, VMEM, VMEM, VMEM),
        scratch_shapes=[
            pltpu.VMEM((4, 2, 4, 256, 256), BF16),
            pltpu.VMEM((2, 256, 256), BF16),
            pltpu.VMEM((2, 256, 256), BF16),
            pltpu.VMEM((2, 128, 256), BF16),
            pltpu.VMEM((2, 128, 256), BF16),
            pltpu.VMEM((8, 24, 128), F32),
            pltpu.VMEM((8, 24, 128), F32),
            pltpu.VMEM((4, 24, 128), F32),
            pltpu.VMEM((24, 128), F32),
            dma((2,)), dma((2,)), dma((2,)), dma((2,)), dma((2,)), dma((2,)), dma((2,)),
            dma((4, 2, 4)), dma((4, 2, 4)), dma((18,)), dma((18,)),
        ],
        compiler_params=pltpu.CompilerParams(collective_id=1, has_side_effects=True, vmem_limit_bytes=48 * 2**20),
        name="reduce",
    )(D, ATT, GQ, BV)


def local(query_rows, key_rows, value_rows, out_grad, destination, group_first):
    ctx = lax.axis_index("ctx")
    linked = (group_first[0, 0] < ctx).astype(jnp.int32)
    lk = jnp.broadcast_to(linked, (1, 1, 128))
    plan = destination.reshape(32, 128)
    blocks = plan // 128
    spots = plan % 128
    ids = jnp.arange(128)
    same = (blocks[:, :, None] == blocks[:, None, :]) & (ids[None, :, None] < ids[None, None, :])
    ranks = jnp.sum(same.astype(jnp.int32), axis=1)
    code = blocks * 8 + ranks
    hits = code[:, :, None] == jnp.arange(256)[None, None, :]
    PP = jnp.sum(jnp.where(hits, spots[:, :, None] + 1, 0), axis=1)
    PP = PP.reshape(32, 32, 8).transpose(1, 0, 2).reshape(32, 1, 256)
    cores = (jnp.arange(32) % 2)[:, None] * 8
    PR = (blocks * 16 + cores + ranks).reshape(16, 1, 256)
    chip = ctx // 2
    mine = lax.dynamic_slice_in_dim(PP.reshape(32, 16, 16), chip, 1, 1)
    PQ = jnp.broadcast_to(jnp.where(mine == 0, 127, mine - 1), (32, 8, 16)).reshape(32, 1, 128)
    KV, QX, GX, LK = gathered(query_rows, key_rows, value_rows, out_grad, lk)
    D, ATT, GQ, BV = attended(chip.reshape(1).astype(jnp.int32), KV, QX, GX, LK, PR, PP, PQ)
    att, gq, gk, gv, BT = reduced(D, ATT, GQ, BV)
    bias = jnp.concatenate([BT[:, :16].reshape(4096), BT[:, 16:18].reshape(512)])
    return att, gq, gk, gv, bias


def solution(mesh):
    rows = P(("dp", "ctx"), None)
    return jax.shard_map(
        local, mesh=mesh, in_specs=(rows, rows, rows, rows, P("dp", None), P("dp", "ctx")),
        out_specs=(rows, rows, rows, rows, P()), check_vma=False)
```

time: 473 us -> 224 us (0.47); the launches traced: 464 us -> 224 us
  Pallas kernels: 0 us -> 202 us
  waiting for transfers between devices: 164 us -> 0 us
  starting transfers between devices: 107 us -> 0 us
  local copies, waits for them, and re-layouts: 90.1 us -> 14.9 us
  blocking collectives: 55.8 us -> 0 us
  matrix products: 21 us -> 0 us
  other arithmetic: 23.5 us -> 5.65 us
    pallas_call x0 -> x3, Pallas kernels: none -> 202 us  [the longest x1 85.2 us: attended(): pl.pallas_call(attention_kernel, out_shape=(jax.ShapeDtypeStruct((2, 2, 8...]
    all_to_all x10 -> x0, waiting for transfers between devices: 164 us -> none  [the longest x1 49.7 us: local(): lax.all_to_all(returning(attended, back_order, heads, wide), 'ctx', split...]
    all_to_all x10 -> x0, starting transfers between devices: 102 us -> none  [the longest x2 25 us: from_everyone(): lax.all_to_all(jnp.broadcast_to(shard[None], (count, *shard.shape)), axis...]
    all_to_all x1 -> x0, blocking collectives: 55.8 us -> none  [local(): lax.all_to_all(queries, 'ctx', split_axis=0, concat_axis=0, tiled=True)]
    gather x17 -> x0, local copies, waits for them, and re-layouts: 32.9 us -> none  [the longest x8 13 us: settle(): return jnp.take(flat, places, axis=0, mode='fill', fill_value=0)]
    dot_general x12 -> x0, matrix products: 21 us -> none  [product(): return jnp.einsum(form, left, right, preferred_element_type=jnp.float32)]
    reshape x17 -> x2, local copies, waits for them, and re-layouts: 22.3 us -> 1.37 us  [the longest x1 0.69 us: local(): PP = PP.reshape(32, 32, 8).transpose(1, 0, 2).reshape(32, 1, 256)]
    scatter x3 -> x0, local copies, waits for them, and re-layouts: 17.9 us -> none  [the longest x1 16 us: local(): jnp.zeros_like(plan).at[plan]]
  transfers between devices with their start and end apart: 12 -> 0, of which waited for: 10 -> 0; matrix products, arithmetic and copies ran while one was open for 20% -> 0% of each run, Pallas kernels for 0% -> 0%
where the time goes in v1:
time: 224 us
  Pallas kernels  202 us (90%)
  local copies, waits for them, and re-layouts  14.9 us (7%)
  other arithmetic  5.65 us (3%)
    pallas_call x1, Pallas kernels, attended(): pl.pallas_call(attention_kernel, out_shape=(jax.ShapeDtypeStruct((2, 2, 8...  85.2 us
    pallas_call x1, Pallas kernels, gathered(): pl.pallas_call(gather_kernel, out_shape=(jax.ShapeDtypeStruct((2, 2, 8, 2...  62.8 us
    pallas_call x1, Pallas kernels, reduced(): pl.pallas_call(reduce_kernel, out_shape=(jax.ShapeDtypeStruct((128, 4096)...  53.6 us
    unnamed x24, local copies, waits for them, and re-layouts  13.2 us

profile of v1, /device:TPU:1, one launch (start us, length us, event | category | flops | bytes accessed | tf_op | source)
XLA Modules:
  0.0 223.6 jit_solution(13299962433996717595)
XLA Ops:
  1.3 0.1 add.89
  1.4 0.7 add_select_fusion.1
  2.2 0.7 convert_reduce_fusion
  2.9 1.4 add_add_fusion.PR
  4.3 0.7 multiply_add_fusion
  5.0 1.4 select_reduce_fusion
  6.4 0.1 copy.16
  6.5 0.1 copy.17
  6.7 0.7 copy.19.PP
  7.4 0.7 copy.20.PQ
  8.1 0.0 copy-start.2
  8.1 1.2 copy-done.2
  9.3 0.0 copy-start.3
  9.3 1.2 copy-done.3
  10.5 0.0 copy-start.6
  10.5 0.9 copy-done.6
  11.4 0.0 copy-start.7
  11.4 0.9 copy-done.7
  12.3 62.8 %gather.1 = (bf16[2,2,8,256,256]{4,3,2,1,0:T(8,128)(2,1)}, bf16[256,2048]{1,0:T(8,128)(2,1)S(1)}, bf16[256,2048]{1,0:T(8,128)(2,1)S(1)}, s32[32,1,128]{2,1,0:T(1,128)S(1)}) custom-call(bf16[128,4096]{1,0:T(8,128)(2,1)S(1)} %copy-done.2, bf16[128,512]{1,0:T(8,128)(2,1)S(1)} %copy-done.6, bf16[128,512]{1,0:T(8,128)(2,1)S(1)} %copy-done.7, ...), custom_call_target="tpu_custom_call" | custom-call | tf_op jit(solution)/shard_map/gather/pallas_call | solution.py:131
  75.2 0.0 copy-start
  75.2 1.0 copy-done
  76.1 0.0 copy-start.1
  76.1 1.0 copy-done.1
  77.1 0.0 copy-start.8
  77.1 0.6 copy-done.8
  77.7 85.2 %attend.1 = (bf16[2,2,8,256,256]{4,3,2,1,0:T(8,128)(2,1)}, bf16[256,2048]{1,0:T(8,128)(2,1)}, bf16[256,2048]{1,0:T(8,128)(2,1)}, f32[24,128]{1,0:T(8,128)}) custom-call(s32[1]{0:T(128)} %bitcast.own, bf16[2,2,8,256,256]{4,3,2,1,0:T(8,128)(2,1)} %get-tuple-element.18.KV, bf16[256,2048]{1,0:T(8,128)(2,1)} %copy-done, bf16[256,2048]{1,0:T(8,128)(2,1)} %copy-done.1, ...), custom_call_target="tpu_custom_call" | custom-call | tf_op jit(solution)/shard_map/attend/pallas_call | solution.py:259
  162.9 0.0 copy-start.4
  162.9 1.2 copy-done.4
  164.1 0.0 copy-start.5
  164.1 1.2 copy-done.5
  165.3 0.0 copy-start.9
  165.3 0.7 copy-done.9
  166.0 53.6 %reduce.1 = (bf16[128,4096]{1,0:T(8,128)(2,1)S(1)}, bf16[128,4096]{1,0:T(8,128)(2,1)S(1)}, bf16[128,512]{1,0:T(8,128)(2,1)S(1)}, bf16[128,512]{1,0:T(8,128)(2,1)S(1)}, f32[2,24,128]{2,1,0:T(8,128)S(1)}) custom-call(bf16[2,2,8,256,256]{4,3,2,1,0:T(8,128)(2,1)} %get-tuple-element.22.D, bf16[256,2048]{1,0:T(8,128)(2,1)S(1)} %copy-done.4, ...), custom_call_target="tpu_custom_call" | custom-call | tf_op jit(solution)/shard_map/reduce/pallas_call | solution.py:428
  219.7 0.6 pad_maximum_fusion
  220.3 1.0 copy.26
  221.3 1.0 copy.27
  222.2 0.7 copy.28
  222.9 0.7 copy.29
  (7 shorter events, 0.1 us)
Async XLA Ops:
  8.1 1.2 copy-start.2
  9.3 1.2 copy-start.3
  10.5 0.9 copy-start.6
  11.4 0.9 copy-start.7
  75.2 1.0 copy-start
  76.1 1.0 copy-start.1
  77.1 0.6 copy-start.8
  162.9 1.2 copy-start.4
  164.1 1.2 copy-start.5
  165.3 0.7 copy-start.9

commit v2 on v0

v2 whole, which is shorter than its diff:
```python
import jax
import jax.numpy as jnp
from jax import lax
from jax.experimental import pallas as pl
from jax.experimental.pallas import tpu as pltpu
from jax.sharding import PartitionSpec as P

MESH = pl.DeviceIdType.MESH
VMEM = pl.BlockSpec(memory_space=pltpu.VMEM)
ANY = pl.BlockSpec(memory_space=pl.ANY)
F32 = jnp.float32
BF16 = jnp.bfloat16


def places():
    dp = lax.axis_index("dp")
    ctx = lax.axis_index("ctx")
    return dp, ctx, ctx // 16, lax.rem(ctx // 2, 8), lax.rem(ctx, 2)


def at_ctx(dp, yh, z, c):
    return (dp, yh * 16 + z * 2 + c)


def cols(start, size):
    return pl.ds(pl.multiple_of(start, 128), size)


SCALE = 128**-0.5
LOG2E = 1.4426950408889634
GROUPS = 4


def dot(a, b, ca, cb):
    return lax.dot_general(a, b, (((ca,), (cb,)), ((), ())), preferred_element_type=F32)


def step_kernel(q, k, v, g, lk, PR, PP, PQ, att, gq, gk, gv, BT,
                KV, QX, GX, LK, QP, GP, OP, DQP, PAD, D, ATT, GQ, BV, R, YS, YR, KS, KR, BZ, BY, BX, BM,
                local_sem, core_send, core_recv, y_send, y_recv, z_send, z_recv, l_send, l_recv,
                out_sem, o_send, o_recv, k_send, k_recv, v_send, v_recv, r_send, r_recv, b_send, b_recv):
    dp, ctx, yh, z, c = places()
    yl, x = dp // 4, lax.rem(dp, 4)
    y = yh * 4 + yl
    other = 1 - c
    half = pl.ds(0, 128), pl.ds(128, 128)
    mine = pl.ds(pl.multiple_of(c * 128, 128), 128)
    theirs = pl.ds(pl.multiple_of(other * 128, 128), 128)
    chip = yh * 8 + z

    def copied(src, dst, sem):
        copy = pltpu.make_async_copy(src, dst, sem)
        copy.start()
        return copy

    local = []
    for gi in range(2):
        at = cols((2 * c + gi) * 128, 128)
        local.append(copied(k.at[:, at], KV.at[gi, yh, z, mine, half[0]], local_sem.at[2 * gi]))
        local.append(copied(v.at[:, at], KV.at[gi, yh, z, mine, half[1]], local_sem.at[2 * gi + 1]))
    local.append(copied(q.at[:, cols(c * 2048, 2048)], QX.at[mine, :], local_sem.at[4]))
    local.append(copied(g.at[:, cols(c * 2048, 2048)], GX.at[mine, :], local_sem.at[5]))
    LK[ctx] = lk[0]

    def at_y(yy):
        return (lax.rem(yy, 4) * 4 + x, (yy // 4) * 16 + z * 2 + c)

    partner = at_ctx(dp, yh, z, other)
    across = at_ctx(dp, 1 - yh, z, c)
    peers = [(dp, lax.rem(ctx + i, 32)) for i in range(1, 32)]
    along_z = [at_ctx(dp, yh, lax.rem(z + i, 8), c) for i in range(1, 8)]
    along_y = [at_y(lax.rem(y + i, 8)) for i in range(1, 8)]
    along_x = [(yl * 4 + lax.rem(x + i, 4), ctx) for i in range(1, 4)]
    right, left = along_z[0], along_z[6]
    barrier = pltpu.get_barrier_semaphore()
    for device in peers + along_y[:3] + along_y[4:] + along_x:
        pl.semaphore_signal(barrier, inc=1, device_id=device, device_id_type=MESH)
    pl.semaphore_wait(barrier, 40)

    sent = []

    def remote(src, dst, send, recv, device):
        copy = pltpu.make_async_remote_copy(src_ref=src, dst_ref=dst, send_sem=send, recv_sem=recv,
                                            device_id=device, device_id_type=MESH)
        copy.start()
        sent.append(copy)
        return copy

    core = []
    for gi in range(2):
        at = cols((2 * other + gi) * 128, 128)
        for j, src in ((0, k), (1, v)):
            i = 2 * gi + j
            core.append(remote(src.at[:, at], KV.at[gi, yh, z, mine, half[j]], core_send.at[i], core_recv.at[i], partner))
    for i, (src, dst) in ((4, (q, QX)), (5, (g, GX))):
        core.append(remote(src.at[:, cols(other * 2048, 2048)], dst.at[mine, :], core_send.at[i], core_recv.at[i],
                           partner))

    def side(far):
        return 1 - yh if far else yh

    def ring(zz):
        return lax.rem(zz + 8, 8)

    def placing(c):
        return (PR[c] == lax.broadcasted_iota(jnp.int32, (512, 256), 0)).astype(BF16)

    def widen(gi, far, zs):
        found = [dot(placing(side(far) * 8 + zz), KV[gi, side(far), zz], 1, 0).astype(BF16) for zz in zs]
        for zz, rows in zip(zs, found):
            at = pl.ds(pl.multiple_of((side(far) * 8 + zz) * 16, 16), 16)
            PAD[gi, 1:33, at, :] = rows.reshape(32, 16, 256)

    rows = {}
    ys = {}

    def bring(gi, far, s):
        item = 2 * far + gi
        if s == 0:
            if far:
                ys[gi].wait_recv()
            else:
                for i in (2 * gi, 2 * gi + 1):
                    local[i].wait()
                    core[i].wait_recv()
        for way in range(2):
            if s > 0:
                rows[(item, way, s - 1)].wait_recv()
            if s < 4:
                ref = KV.at[gi, side(far), ring(z - s if way == 0 else z + s)]
                if s == 3:
                    ref = ref.at[half[way], :]
                rows[(item, way, s)] = remote(ref, ref, z_send.at[item, way, s], z_recv.at[item, way, s],
                                              right if way == 0 else left)
        if s == 0 and not far:
            ref = KV.at[gi, yh, z]
            ys[gi] = remote(ref, ref, y_send.at[gi], y_recv.at[gi], across)
        widen(gi, far, [ring(z + s)] if s in (0, 4) else [ring(z - s), ring(z + s)])

    def queries(ref, gi, b):
        at = slice(b * 16 + 16, b * 16 + 32)
        return jnp.concatenate([ref[at, (gi * 8 + h) * 128:(gi * 8 + h + 1) * 128] for h in range(8)], axis=0)

    def seat(b):
        return (PP[b] == lax.broadcasted_iota(jnp.int32, (128, 256), 0) + 1).astype(BF16)

    def unseat(gi, dk, dv, b):
        grads = [jnp.concatenate([dk[j], dv[j]], axis=1).astype(BF16) for j in range(len(b))]
        back = [dot(seat(b[j]), grads[j], 0, 0).astype(BF16) for j in range(len(b))]
        for j in range(len(b)):
            PAD[gi, b[j] + 1] = back[j]

    def blocks(gi, i, carry):
        s_last, p_last, w_last, sl_last, kv_last, total = carry
        un = 32 // GROUPS
        span = range(un)
        b = [i * un + j for j in span]
        kv = [dot(seat(b[j]), PAD[gi, b[j] + 1], 1, 0).astype(BF16) for j in span]
        qs = [queries(QP, gi, b[0] + j - 1) for j in range(un + 2)]
        os = [queries(GP, gi, b[0] + j - 1) for j in range(un + 2)]
        s = [dot(kv[j][:, 0:128], jnp.concatenate([qs[j + 1], qs[j + 2]], axis=0), 1, 1) for j in span]
        p = [dot(kv[j][:, 128:256], jnp.concatenate([os[j + 1], os[j + 2]], axis=0), 1, 1) for j in span]
        u = lax.broadcasted_iota(jnp.int32, (128, 128), 0)
        s_own = [jnp.where(u <= PQ[b[j]], s[j][:, 0:128], -jnp.inf) for j in span]
        s_pri = [jnp.where(jnp.broadcast_to(LK[b[j]] > 0, (128, 128)), s[j - 1][:, 128:256] if j else s_last, -jnp.inf)
                 for j in span]
        p_own = [p[j][:, 0:128] for j in span]
        p_pri = [p[j - 1][:, 128:256] if j else p_last for j in span]
        top = [jnp.max(jnp.maximum(s_own[j], s_pri[j]), axis=0, keepdims=True) for j in span]
        e_own = [jnp.exp2((s_own[j] - top[j]) * (SCALE * LOG2E)) for j in span]
        e_pri = [jnp.exp2((s_pri[j] - top[j]) * (SCALE * LOG2E)) for j in span]
        inv = [1.0 / jnp.sum(e_own[j] + e_pri[j], axis=0, keepdims=True) for j in span]
        w_own = [e_own[j] * inv[j] for j in span]
        w_pri = [e_pri[j] * inv[j] for j in span]
        centred = [jnp.sum(w_own[j] * p_own[j] + w_pri[j] * p_pri[j], axis=0, keepdims=True) for j in span]
        sl_own = [((w_own[j] * (p_own[j] - centred[j])) * SCALE).astype(BF16) for j in span]
        sl_pri = [((w_pri[j] * (p_pri[j] - centred[j])) * SCALE).astype(BF16) for j in span]
        w_own = [w.astype(BF16) for w in w_own]
        w_pri = [w.astype(BF16) for w in w_pri]
        att, gq, dk, dv = [], [], [], []
        for j in span:
            pair = jnp.concatenate([kv[j - 1] if j else kv_last, kv[j]], axis=0)
            att.append(dot(jnp.concatenate([w_pri[j], w_own[j]], axis=0), pair[:, 128:256], 0, 0).astype(BF16))
            gq.append(dot(jnp.concatenate([sl_pri[j], sl_own[j]], axis=0), pair[:, 0:128], 0, 0).astype(BF16))
            dk.append(dot(jnp.concatenate([sl_own[j - 1] if j else sl_last, sl_pri[j]], axis=1),
                          jnp.concatenate([qs[j], qs[j + 1]], axis=0), 1, 0))
            dv.append(dot(jnp.concatenate([w_own[j - 1] if j else w_last, w_pri[j]], axis=1),
                          jnp.concatenate([os[j], os[j + 1]], axis=0), 1, 0))
        for j in span:
            at = slice(b[j] * 16, b[j] * 16 + 16)
            for h in range(8):
                to = slice((gi * 8 + h) * 128, (gi * 8 + h + 1) * 128)
                OP[at, to] = att[j][h * 16:(h + 1) * 16]
                DQP[at, to] = gq[j][h * 16:(h + 1) * 16]
        first = 0 if i else 1
        unseat(gi, dk[first:], dv[first:], [bj - 1 for bj in b[first:]])
        for j in span[first:]:
            total = total + jnp.sum(dv[j].reshape(16, 8, 128), axis=0)
        if i == GROUPS - 1:
            dk = dot(sl_own[-1], qs[un], 1, 0)
            dv = dot(w_own[-1], os[un], 1, 0)
            unseat(gi, [dk], [dv], [31])
            total = total + jnp.sum(dv.reshape(16, 8, 128), axis=0)
            BV[16 + gi:17 + gi, :] = jnp.sum(total, axis=0, keepdims=True)
        return s[-1][:, 128:256], p[-1][:, 128:256], w_own[-1], sl_own[-1], kv[-1], total

    def opening():
        zf = jnp.zeros((128, 128), F32)
        zb = jnp.zeros((128, 128), BF16)
        return zf, zf, zb, zb, jnp.zeros((128, 256), BF16), jnp.zeros((8, 128), F32)

    def narrow(gi, places):
        out = []
        for far, zz in places:
            at = pl.ds(pl.multiple_of((side(far) * 8 + zz) * 16, 16), 16)
            wide = PAD[gi, 1:33, at, :].reshape(512, 256)
            out.append(dot(placing(side(far) * 8 + zz), wide, 0, 0).astype(BF16))
        for (far, zz), value in zip(places, out):
            D[gi, side(far), zz] = value

    back = {}

    def give(gi, far, s):
        item = 2 * far + gi
        for way in range(2):
            target = z + 4 - s if way == 0 else z - 4 + s
            term = D.at[gi, side(far), ring(target)]
            dst = R.at[item, way, s]
            if s == 0:
                src = term.at[half[way], :]
                dst = dst.at[half[way], :]
            else:
                back[(item, way, s - 1)].wait_recv()
                src = R.at[item, way, s - 1]
                for part in range(2):
                    at = slice(part * 128, part * 128 + 128)
                    if s == 1 and part != way:
                        src[at, :] = term[at, :]
                    else:
                        src[at, :] = (src[at, :].astype(F32) + term[at, :].astype(F32)).astype(BF16)
            back[(item, way, s)] = remote(src, dst, r_send.at[item, way, s], r_recv.at[item, way, s],
                                          right if way == 0 else left)

    def total(gi, far, at):
        item = 2 * far + gi
        return (D[gi, side(far), z, at, :].astype(F32) + R[item, 0, 3, at, :].astype(F32)
                + R[item, 1, 3, at, :].astype(F32))

    def finish(gi, far):
        item = 2 * far + gi
        back[(item, 0, 3)].wait_recv()
        back[(item, 1, 3)].wait_recv()
        if far:
            YS[gi] = total(gi, 1, slice(0, 256)).astype(BF16)
            ys[gi] = remote(YS.at[gi], YR.at[gi], v_send.at[gi], v_recv.at[gi], across)
            return
        ys[gi].wait_recv()
        KS[gi] = (total(gi, 0, theirs) + YR[gi, theirs, :].astype(F32)).astype(BF16)
        ks.append(remote(KS.at[gi], KR.at[gi], k_send.at[gi], k_recv.at[gi], partner))
        done = (total(gi, 0, mine) + YR[gi, mine, :].astype(F32)).astype(BF16)
        gk[:, cols((2 * c + gi) * 128, 128)] = done[:, 0:128]
        gv[:, cols((2 * c + gi) * 128, 128)] = done[:, 128:256]

    def start_reduce(gi):
        narrow(gi, [(1, ring(z + 4)), (0, ring(z + 4))])
        give(gi, 1, 0)
        give(gi, 0, 0)
        narrow(gi, [(far, ring(z + i)) for i in (3, 5) for far in (1, 0)])
        narrow(gi, [(far, ring(z + i)) for i in (2, 6) for far in (1, 0)])
        narrow(gi, [(far, ring(z + i)) for i in (1, 7) for far in (1, 0)])
        narrow(gi, [(far, z) for far in (1, 0)])

    ks = []
    BV[...] = jnp.zeros_like(BV)
    zeros = jnp.zeros((16, 2048), BF16)
    for ref in (QP, GP):
        ref[0:16, :] = zeros
        ref[528:544, :] = zeros

    bring(0, 0, 0)
    bring(1, 0, 0)
    flags = [remote(lk.at[0], LK.at[ctx], l_send.at[i], l_recv.at[i], peers[i]) for i in range(31)]
    for i in (4, 5):
        local[i].wait()
        core[i].wait_recv()
    here = placing(chip)

    def spread(ref, src, j):
        at = slice(j * 256, (j + 1) * 256)
        ref[16:528, at] = dot(here, src[:, at], 1, 0).astype(BF16)

    for j in range(4):
        spread(QP, QX, j)
    bring(0, 0, 1)
    for j in range(4):
        spread(GP, GX, j)
    bring(0, 1, 0)
    for j in range(4, 8):
        spread(QP, QX, j)
    bring(0, 0, 2)
    for j in range(4, 8):
        spread(GP, GX, j)
    bring(0, 1, 1)
    bring(0, 0, 3)
    bring(0, 1, 2)
    bring(0, 0, 4)
    bring(1, 0, 1)
    bring(0, 1, 3)
    bring(1, 1, 0)
    for copy in flags:
        copy.wait_recv()
    bring(0, 1, 4)

    carry = blocks(0, 0, opening())
    bring(1, 0, 2)
    bring(1, 1, 1)
    carry = blocks(0, 1, carry)
    bring(1, 0, 3)
    carry = blocks(0, 2, carry)
    bring(1, 1, 2)
    carry = blocks(0, 3, carry)
    bring(1, 0, 4)
    start_reduce(0)
    bring(1, 1, 3)
    give(0, 1, 1)
    bring(1, 1, 4)
    carry = blocks(1, 0, opening())
    give(0, 0, 1)
    carry = blocks(1, 1, carry)
    give(0, 1, 2)
    carry = blocks(1, 2, carry)
    give(0, 0, 2)
    carry = blocks(1, 3, carry)
    start_reduce(1)
    give(0, 1, 3)
    here = placing(chip)
    for j in range(8):
        at = slice(j * 256, (j + 1) * 256)
        ATT[:, at] = dot(here, OP[:, at], 0, 0).astype(BF16)
        wide = dot(here, DQP[:, at], 0, 0)
        GQ[:, at] = wide.astype(BF16)
        sums = jnp.sum(wide, axis=0, keepdims=True)
        BV[2 * j:2 * j + 1, :] = sums[:, 0:128]
        BV[2 * j + 1:2 * j + 2, :] = sums[:, 128:256]
    give(0, 0, 3)
    outs = []
    for i, (src, dst) in enumerate(((ATT, att), (GQ, gq))):
        outs.append(copied(src.at[mine, :], dst.at[:, cols(c * 2048, 2048)], out_sem.at[i]))
        core.append(remote(src.at[theirs, :], dst.at[:, cols(c * 2048, 2048)], o_send.at[i], o_recv.at[i], partner))

    def share(buffer, place, line, base, value):
        buffer[place] = value
        return [remote(buffer.at[place], buffer.at[place], b_send.at[base + i], b_recv.at[base + i], device)
                for i, device in enumerate(line)]

    def summed(buffer, copies, count):
        for copy in copies:
            copy.wait_recv()
        value = buffer[0]
        for i in range(1, count):
            value = value + buffer[i]
        return value

    copies = share(BZ, z, along_z, 0, BV[...])
    give(1, 1, 1)
    finish(0, 1)
    copies = share(BY, y, along_y, 7, summed(BZ, copies, 8))
    give(1, 0, 1)
    give(1, 1, 2)
    copies = share(BX, x, along_x, 14, summed(BY, copies, 8))
    finish(0, 0)
    give(1, 0, 2)
    give(1, 1, 3)
    BM[...] = summed(BX, copies, 4) * (65536.0**-0.5)
    BT[c] = BM[...]
    last = remote(BM, BT.at[c], b_send.at[17], b_recv.at[17], partner)
    give(1, 0, 3)
    finish(1, 1)
    finish(1, 0)
    for gi in range(2):
        ks[gi].wait_recv()
        gk[:, cols((2 * other + gi) * 128, 128)] = KR[gi, :, 0:128]
        gv[:, cols((2 * other + gi) * 128, 128)] = KR[gi, :, 128:256]
    last.wait_recv()
    for copy in core[6:]:
        copy.wait_recv()
    for copy in outs:
        copy.wait()
    for copy in sent:
        copy.wait_send()


def stepped(q, k, v, g, lk, PR, PP, PQ):
    dma = pltpu.SemaphoreType.DMA
    return pl.pallas_call(
        step_kernel,
        out_shape=(
            jax.ShapeDtypeStruct((128, 4096), BF16),
            jax.ShapeDtypeStruct((128, 4096), BF16),
            jax.ShapeDtypeStruct((128, 512), BF16),
            jax.ShapeDtypeStruct((128, 512), BF16),
            jax.ShapeDtypeStruct((2, 24, 128), F32),
        ),
        in_specs=[ANY] * 4 + [VMEM] * 4,
        out_specs=(ANY, ANY, VMEM, VMEM, VMEM),
        scratch_shapes=[
            pltpu.VMEM((2, 2, 8, 256, 256), BF16),
            pltpu.VMEM((256, 2048), BF16),
            pltpu.VMEM((256, 2048), BF16),
            pltpu.VMEM((32, 1, 128), jnp.int32),
            pltpu.VMEM((544, 2048), BF16),
            pltpu.VMEM((544, 2048), BF16),
            pltpu.VMEM((512, 2048), BF16),
            pltpu.VMEM((512, 2048), BF16),
            pltpu.VMEM((2, 33, 256, 256), BF16),
            pltpu.VMEM((2, 2, 8, 256, 256), BF16),
            pltpu.VMEM((256, 2048), BF16),
            pltpu.VMEM((256, 2048), BF16),
            pltpu.VMEM((24, 128), F32),
            pltpu.VMEM((4, 2, 4, 256, 256), BF16),
            pltpu.VMEM((2, 256, 256), BF16),
            pltpu.VMEM((2, 256, 256), BF16),
            pltpu.VMEM((2, 128, 256), BF16),
            pltpu.VMEM((2, 128, 256), BF16),
            pltpu.VMEM((8, 24, 128), F32),
            pltpu.VMEM((8, 24, 128), F32),
            pltpu.VMEM((4, 24, 128), F32),
            pltpu.VMEM((24, 128), F32),
            dma((6,)), dma((6,)), dma((6,)), dma((2,)), dma((2,)), dma((4, 2, 4)), dma((4, 2, 4)), dma((31,)), dma((31,)),
            dma((2,)), dma((2,)), dma((2,)), dma((2,)), dma((2,)), dma((2,)), dma((2,)), dma((4, 2, 4)), dma((4, 2, 4)),
            dma((18,)), dma((18,)),
        ],
        compiler_params=pltpu.CompilerParams(collective_id=0, has_side_effects=True, vmem_limit_bytes=62 * 2**20),
        name="step",
    )(q, k, v, g, lk, PR, PP, PQ)


def local(query_rows, key_rows, value_rows, out_grad, destination, group_first):
    ctx = lax.axis_index("ctx")
    linked = (group_first[0, 0] < ctx).astype(jnp.int32)
    lk = jnp.broadcast_to(linked, (1, 1, 128))
    plan = destination.reshape(32, 128)
    blocks = plan // 128
    spots = plan % 128
    ids = jnp.arange(128)
    same = (blocks[:, :, None] == blocks[:, None, :]) & (ids[None, :, None] < ids[None, None, :])
    ranks = jnp.sum(same.astype(jnp.int32), axis=1)
    code = blocks * 8 + ranks
    hits = code[:, :, None] == jnp.arange(256)[None, None, :]
    PP = jnp.sum(jnp.where(hits, spots[:, :, None] + 1, 0), axis=1)
    PP = PP.reshape(32, 32, 8).transpose(1, 0, 2).reshape(32, 1, 256)
    cores = (jnp.arange(32) % 2)[:, None] * 8
    PR = (blocks * 16 + cores + ranks).reshape(16, 1, 256)
    chip = ctx // 2
    mine = lax.dynamic_slice_in_dim(PP.reshape(32, 16, 16), chip, 1, 1)
    PQ = jnp.broadcast_to(jnp.where(mine == 0, 127, mine - 1), (32, 8, 16)).reshape(32, 1, 128)
    att, gq, gk, gv, BT = stepped(query_rows, key_rows, value_rows, out_grad, lk, PR, PP, PQ)
    bias = jnp.concatenate([BT[:, :16].reshape(4096), BT[:, 16:18].reshape(512)])
    return att, gq, gk, gv, bias


def solution(mesh):
    rows = P(("dp", "ctx"), None)
    return jax.shard_map(
        local, mesh=mesh, in_specs=(rows, rows, rows, rows, P("dp", None), P("dp", "ctx")),
        out_specs=(rows, rows, rows, rows, P()), check_vma=False)
```

time: 473 us -> 132 us (0.28); the launches traced: 464 us -> 132 us
  waiting for transfers between devices: 164 us -> 0 us
  Pallas kernels: 0 us -> 117 us
  starting transfers between devices: 107 us -> 0 us
  local copies, waits for them, and re-layouts: 90.1 us -> 8.3 us
  blocking collectives: 55.8 us -> 0 us
  matrix products: 21 us -> 0 us
  other arithmetic: 23.5 us -> 4.98 us
    all_to_all x10 -> x0, waiting for transfers between devices: 164 us -> none  [the longest x1 49.7 us: local(): lax.all_to_all(returning(attended, back_order, heads, wide), 'ctx', split...]
    pallas_call x0 -> x1, Pallas kernels: none -> 117 us  [stepped(): pl.pallas_call(step_kernel, out_shape=(jax.ShapeDtypeStruct((128, 4096),...]
    all_to_all x10 -> x0, starting transfers between devices: 102 us -> none  [the longest x2 25 us: from_everyone(): lax.all_to_all(jnp.broadcast_to(shard[None], (count, *shard.shape)), axis...]
    all_to_all x1 -> x0, blocking collectives: 55.8 us -> none  [local(): lax.all_to_all(queries, 'ctx', split_axis=0, concat_axis=0, tiled=True)]
    gather x17 -> x0, local copies, waits for them, and re-layouts: 32.9 us -> none  [the longest x8 13 us: settle(): return jnp.take(flat, places, axis=0, mode='fill', fill_value=0)]
    dot_general x12 -> x0, matrix products: 21 us -> none  [product(): return jnp.einsum(form, left, right, preferred_element_type=jnp.float32)]
    reshape x17 -> x2, local copies, waits for them, and re-layouts: 22.3 us -> 1.37 us  [the longest x1 0.69 us: local(): PP = PP.reshape(32, 32, 8).transpose(1, 0, 2).reshape(32, 1, 256)]
    scatter x3 -> x0, local copies, waits for them, and re-layouts: 17.9 us -> none  [the longest x1 16 us: local(): jnp.zeros_like(plan).at[plan]]
  transfers between devices with their start and end apart: 12 -> 0, of which waited for: 10 -> 0; matrix products, arithmetic and copies ran while one was open for 20% -> 0% of each run, Pallas kernels for 0% -> 0%
where the time goes in v2:
time: 132 us
  Pallas kernels  117 us (89%)
  local copies, waits for them, and re-layouts  8.3 us (6%)
  other arithmetic  4.98 us (4%)
  between operations  1.39 us (1%)
    pallas_call x1, Pallas kernels, stepped(): pl.pallas_call(step_kernel, out_shape=(jax.ShapeDtypeStruct((128, 4096),...  117 us
    unnamed x12, local copies, waits for them, and re-layouts  4.7 us

profile of v2, /device:TPU:1, one launch (start us, length us, event | category | flops | bytes accessed | tf_op | source)
XLA Modules:
  0.0 131.7 jit_solution(11247717022765935360)
XLA Ops:
  0.6 0.0 copy-start.1
  0.7 0.8 add_select_fusion.1
  1.5 0.7 convert_reduce_fusion
  2.2 0.7 multiply_add_fusion
  2.9 1.4 %select_reduce_fusion = s32[32,256]{1,0:T(8,128)S(1)} fusion(s32[32,128]{1,0:T(8,128)S(1)} %get-tuple-element.16, s32[32,128]{1,0:T(8,128)S(1)} %get-tuple-element.15), kind=kLoop, calls=%fused_computation | loop fusion | flops 3137536 | bytes 65536 | tf_op jit(solution)/shard_map/reduce_sum | solution.py:450
  4.3 0.1 copy.16
  4.4 0.1 copy.17
  4.6 0.7 copy.20.PQ
  5.3 0.7 copy.19.PP
  6.6 0.5 broadcast_in_dim.34.lk
  7.1 0.1 add.89
  7.2 0.0 copy-done.1
  7.2 0.7 add_add_fusion.PR
  7.9 117.0 %step.1 = (bf16[128,4096]{1,0:T(8,128)(2,1)}, bf16[128,4096]{1,0:T(8,128)(2,1)}, bf16[128,512]{1,0:T(8,128)(2,1)}, bf16[128,512]{1,0:T(8,128)(2,1)}, f32[2,24,128]{2,1,0:T(8,128)}) custom-call(bf16[128,4096]{1,0:T(8,128)(2,1)} %q.1, bf16[128,512]{1,0:T(8,128)(2,1)} %k.1, bf16[128,512]{1,0:T(8,128)(2,1)} %v.1, bf16[128,4096]{1,0:T(8,128)(2,1)} %g.1, ...), custom_call_target="tpu_custom_call" | custom-call | tf_op jit(solution)/shard_map/step/pallas_call | solution.py:395
  125.0 0.7 slice.6
  125.7 0.7 slice.7
  126.4 0.6 pad_maximum_fusion
  127.0 0.0 copy-start
  127.0 2.4 %copy.26 = bf16[128,4096]{1,0:T(8,128)(2,1)} copy(bf16[128,4096]{1,0:T(8,128)(2,1)} %get-tuple-element.22) | data formatting | bytes 2097152
  129.4 0.0 copy-done
  129.4 0.0 copy-start.3
  129.4 0.0 copy-start.2
  129.4 1.0 copy.27
  130.3 0.0 copy-done.3
  130.4 0.7 copy.28
  131.0 0.0 copy-done.2
  131.0 0.7 copy.29
  (4 shorter events, 0.0 us)
Async XLA Ops:
  0.6 6.6 %copy-start.1 = (s32[1,4096]{1,0:T(1,128)S(1)}, s32[1,4096]{1,0:T(1,128)}, u32[]{:S(2)}) copy-start(s32[1,4096]{1,0:T(1,128)} %param.10) | copy-start | bytes 49156
  127.0 2.4 %copy-start = (bf16[128,4096]{1,0:T(8,128)(2,1)S(1)}, bf16[128,4096]{1,0:T(8,128)(2,1)}, u32[]{:S(2)}) copy-start(bf16[128,4096]{1,0:T(8,128)(2,1)} %get-tuple-element.23) | copy-start | bytes 3145732
  129.4 1.0 copy-start.3
  129.4 1.7 %copy-start.2 = (bf16[128,512]{1,0:T(8,128)(2,1)S(1)}, bf16[128,512]{1,0:T(8,128)(2,1)}, u32[]{:S(2)}) copy-start(bf16[128,512]{1,0:T(8,128)(2,1)} %get-tuple-element.25) | copy-start | bytes 393220

commit v3 on v2

--- a/solution.py
+++ b/solution.py
@@ -8,6 +8,8 @@
 MESH = pl.DeviceIdType.MESH
 VMEM = pl.BlockSpec(memory_space=pltpu.VMEM)
 ANY = pl.BlockSpec(memory_space=pl.ANY)
+HBM = pl.BlockSpec(memory_space=pltpu.HBM)
+LIMIT = 62
 F32 = jnp.float32
 BF16 = jnp.bfloat16
 
@@ -35,8 +37,8 @@
     return lax.dot_general(a, b, (((ca,), (cb,)), ((), ())), preferred_element_type=F32)
 
 
-def step_kernel(q, k, v, g, lk, PR, PP, PQ, att, gq, gk, gv, BT,
-                KV, QX, GX, LK, QP, GP, OP, DQP, PAD, D, ATT, GQ, BV, R, YS, YR, KS, KR, BZ, BY, BX, BM,
+def step_kernel(q, k, v, g, plan, first, att, gq, gk, gv, bias,
+                KV, QX, GX, LK, PS, PP, PQ, BT, QP, GP, OP, DQP, PAD, D, ATT, GQ, BV, R, YS, YR, KS, KR, BZ, BY, BX, BM,
                 local_sem, core_send, core_recv, y_send, y_recv, z_send, z_recv, l_send, l_recv,
                 out_sem, o_send, o_recv, k_send, k_recv, v_send, v_recv, r_send, r_recv, b_send, b_recv):
     dp, ctx, yh, z, c = places()
@@ -60,22 +62,22 @@
         local.append(copied(v.at[:, at], KV.at[gi, yh, z, mine, half[1]], local_sem.at[2 * gi + 1]))
     local.append(copied(q.at[:, cols(c * 2048, 2048)], QX.at[mine, :], local_sem.at[4]))
     local.append(copied(g.at[:, cols(c * 2048, 2048)], GX.at[mine, :], local_sem.at[5]))
-    LK[ctx] = lk[0]
+    flag = c * 16 + yh * 8 + z
+    LK[flag] = (jnp.broadcast_to(first[...], (1, 128)) < ctx).astype(jnp.int32)
 
     def at_y(yy):
         return (lax.rem(yy, 4) * 4 + x, (yy // 4) * 16 + z * 2 + c)
 
     partner = at_ctx(dp, yh, z, other)
     across = at_ctx(dp, 1 - yh, z, c)
-    peers = [(dp, lax.rem(ctx + i, 32)) for i in range(1, 32)]
     along_z = [at_ctx(dp, yh, lax.rem(z + i, 8), c) for i in range(1, 8)]
     along_y = [at_y(lax.rem(y + i, 8)) for i in range(1, 8)]
     along_x = [(yl * 4 + lax.rem(x + i, 4), ctx) for i in range(1, 4)]
     right, left = along_z[0], along_z[6]
     barrier = pltpu.get_barrier_semaphore()
-    for device in peers + along_y[:3] + along_y[4:] + along_x:
+    for device in along_z + along_y + along_x + [partner]:
         pl.semaphore_signal(barrier, inc=1, device_id=device, device_id_type=MESH)
-    pl.semaphore_wait(barrier, 40)
+    pl.semaphore_wait(barrier, 18)
 
     sent = []
 
@@ -103,7 +105,38 @@
         return lax.rem(zz + 8, 8)
 
     def placing(c):
-        return (PR[c] == lax.broadcasted_iota(jnp.int32, (512, 256), 0)).astype(BF16)
+        at = lax.broadcasted_iota(jnp.int32, (512, 128), 0)
+        return jnp.concatenate([(PS[pl.ds(2 * c + i, 1), :] == at).astype(BF16) for i in range(2)], axis=1)
+
+    def tables():
+        def iota(shape, dim):
+            return lax.broadcasted_iota(jnp.int32, shape, dim)
+
+        block = plan[...] // 128
+        spot = plan[...] - block * 128
+        found = jnp.concatenate([block, spot + 1], axis=0).astype(F32)
+        found = jnp.concatenate([found, jnp.zeros((64, 128), F32)], axis=0).T.astype(BF16)
+        lane = iota((128, 1024), 1)
+        device = (iota((128, 1024), 0) == lane // 32).astype(BF16)
+        inside = dot(found, device, 1, 0) == (lane % 32).astype(F32)
+        member = inside.astype(BF16)
+        earlier = dot((iota((128, 128), 0) > iota((128, 128), 1)).astype(BF16), member, 1, 0)
+        ranks = dot(jnp.where(inside, earlier, 0.0).astype(BF16), device, 1, 1)
+        PS[...] = block * 16 + iota((32, 128), 0) % 2 * 8 + ranks.T[0:32].astype(jnp.int32)
+        lane = iota((128, 256), 1)
+        row = iota((128, 256), 0)
+        rank = dot(ranks.astype(BF16), (row == lane // 8).astype(BF16), 1, 0)
+        value = dot(found, (row == lane // 8 + 32).astype(BF16), 1, 0)
+        filled = jnp.where(rank == (lane % 8).astype(F32), value, 0.0).astype(BF16)
+        every = dot(member, filled, 0, 0)
+        lane = iota((32, 256), 1) // 8
+        table = jnp.zeros((32, 256), F32)
+        for i in range(32):
+            table = table + jnp.where(lane == i, every[i * 32:i * 32 + 32], 0.0)
+        PP[...] = table.astype(jnp.int32)
+        own = (iota((256, 128), 0) == chip * 16 + iota((256, 128), 1) % 16).astype(BF16)
+        own = dot(table.astype(BF16), own, 1, 0).astype(jnp.int32)
+        PQ[...] = jnp.where(own == 0, 127, own - 1)
 
     def widen(gi, far, zs):
         found = [dot(placing(side(far) * 8 + zz), KV[gi, side(far), zz], 1, 0).astype(BF16) for zz in zs]
@@ -114,7 +147,7 @@
     rows = {}
     ys = {}
 
-    def bring(gi, far, s):
+    def bring(gi, far, s, later=False):
         item = 2 * far + gi
         if s == 0:
             if far:
@@ -135,14 +168,15 @@
         if s == 0 and not far:
             ref = KV.at[gi, yh, z]
             ys[gi] = remote(ref, ref, y_send.at[gi], y_recv.at[gi], across)
-        widen(gi, far, [ring(z + s)] if s in (0, 4) else [ring(z - s), ring(z + s)])
+        if not later:
+            widen(gi, far, [ring(z + s)] if s in (0, 4) else [ring(z - s), ring(z + s)])
 
     def queries(ref, gi, b):
         at = slice(b * 16 + 16, b * 16 + 32)
         return jnp.concatenate([ref[at, (gi * 8 + h) * 128:(gi * 8 + h + 1) * 128] for h in range(8)], axis=0)
 
     def seat(b):
-        return (PP[b] == lax.broadcasted_iota(jnp.int32, (128, 256), 0) + 1).astype(BF16)
+        return (PP[b:b + 1, :] == lax.broadcasted_iota(jnp.int32, (128, 256), 0) + 1).astype(BF16)
 
     def unseat(gi, dk, dv, b):
         grads = [jnp.concatenate([dk[j], dv[j]], axis=1).astype(BF16) for j in range(len(b))]
@@ -161,8 +195,8 @@
         s = [dot(kv[j][:, 0:128], jnp.concatenate([qs[j + 1], qs[j + 2]], axis=0), 1, 1) for j in span]
         p = [dot(kv[j][:, 128:256], jnp.concatenate([os[j + 1], os[j + 2]], axis=0), 1, 1) for j in span]
         u = lax.broadcasted_iota(jnp.int32, (128, 128), 0)
-        s_own = [jnp.where(u <= PQ[b[j]], s[j][:, 0:128], -jnp.inf) for j in span]
-        s_pri = [jnp.where(jnp.broadcast_to(LK[b[j]] > 0, (128, 128)), s[j - 1][:, 128:256] if j else s_last, -jnp.inf)
+        s_own = [jnp.where(u <= PQ[b[j]:b[j] + 1, :], s[j][:, 0:128], -jnp.inf) for j in span]
+        s_pri = [jnp.where(jnp.broadcast_to(LK[seen_at(b[j])] > 0, (128, 128)), s[j - 1][:, 128:256] if j else s_last, -jnp.inf)
                  for j in span]
         p_own = [p[j][:, 0:128] for j in span]
         p_pri = [p[j - 1][:, 128:256] if j else p_last for j in span]
@@ -204,6 +238,9 @@
             BV[16 + gi:17 + gi, :] = jnp.sum(total, axis=0, keepdims=True)
         return s[-1][:, 128:256], p[-1][:, 128:256], w_own[-1], sl_own[-1], kv[-1], total
 
+    def seen_at(b):
+        return b % 2 * 16 + b // 16 * 8 + b // 2 % 8
+
     def opening():
         zf = jnp.zeros((128, 128), F32)
         zb = jnp.zeros((128, 128), BF16)
@@ -271,15 +308,18 @@
         narrow(gi, [(far, z) for far in (1, 0)])
 
     ks = []
+
+    bring(0, 0, 0, later=True)
+    bring(1, 0, 0, later=True)
+    flags = [remote(LK.at[flag], LK.at[flag], l_send.at[i], l_recv.at[i], along_z[i]) for i in range(7)]
+    tables()
     BV[...] = jnp.zeros_like(BV)
     zeros = jnp.zeros((16, 2048), BF16)
     for ref in (QP, GP):
         ref[0:16, :] = zeros
         ref[528:544, :] = zeros
-
-    bring(0, 0, 0)
-    bring(1, 0, 0)
-    flags = [remote(lk.at[0], LK.at[ctx], l_send.at[i], l_recv.at[i], peers[i]) for i in range(31)]
+    for gi in range(2):
+        widen(gi, 0, [z])
     for i in (4, 5):
         local[i].wait()
         core[i].wait_recv()
@@ -292,47 +332,53 @@
     for j in range(4):
         spread(QP, QX, j)
     bring(0, 0, 1)
+    for copy in flags:
+        copy.wait_recv()
+    part = pl.ds(c * 16 + yh * 8, 8)
+    flag_y = remote(LK.at[part], LK.at[part], l_send.at[7], l_recv.at[7], across)
     for j in range(4):
         spread(GP, GX, j)
+    bring(1, 0, 1)
     bring(0, 1, 0)
     for j in range(4, 8):
         spread(QP, QX, j)
+    flag_y.wait_recv()
+    part = pl.ds(c * 16, 16)
+    flag_core = remote(LK.at[part], LK.at[part], l_send.at[8], l_recv.at[8], partner)
     bring(0, 0, 2)
     for j in range(4, 8):
         spread(GP, GX, j)
     bring(0, 1, 1)
     bring(0, 0, 3)
     bring(0, 1, 2)
+    bring(1, 1, 0)
+    bring(0, 1, 3)
+    bring(1, 0, 2)
+    flag_core.wait_recv()
     bring(0, 0, 4)
-    bring(1, 0, 1)
-    bring(0, 1, 3)
-    bring(1, 1, 0)
-    for copy in flags:
-        copy.wait_recv()
     bring(0, 1, 4)
-
+    bring(1, 1, 1)
     carry = blocks(0, 0, opening())
-    bring(1, 0, 2)
-    bring(1, 1, 1)
+    bring(1, 0, 3)
     carry = blocks(0, 1, carry)
-    bring(1, 0, 3)
+    bring(1, 1, 2)
     carry = blocks(0, 2, carry)
-    bring(1, 1, 2)
+    bring(1, 0, 4)
     carry = blocks(0, 3, carry)
-    bring(1, 0, 4)
+    bring(1, 1, 3)
     start_reduce(0)
-    bring(1, 1, 3)
+    bring(1, 1, 4)
     give(0, 1, 1)
-    bring(1, 1, 4)
+    give(0, 0, 1)
     carry = blocks(1, 0, opening())
-    give(0, 0, 1)
+    give(0, 1, 2)
     carry = blocks(1, 1, carry)
-    give(0, 1, 2)
+    give(0, 0, 2)
     carry = blocks(1, 2, carry)
-    give(0, 0, 2)
+    give(0, 1, 3)
     carry = blocks(1, 3, carry)
     start_reduce(1)
-    give(0, 1, 3)
+    give(0, 0, 3)
     here = placing(chip)
     for j in range(8):
         at = slice(j * 256, (j + 1) * 256)
@@ -342,7 +388,7 @@
         sums = jnp.sum(wide, axis=0, keepdims=True)
         BV[2 * j:2 * j + 1, :] = sums[:, 0:128]
         BV[2 * j + 1:2 * j + 2, :] = sums[:, 128:256]
-    give(0, 0, 3)
+    give(1, 1, 1)
     outs = []
     for i, (src, dst) in enumerate(((ATT, att), (GQ, gq))):
         outs.append(copied(src.at[mine, :], dst.at[:, cols(c * 2048, 2048)], out_sem.at[i]))
@@ -362,26 +408,28 @@
         return value
 
     copies = share(BZ, z, along_z, 0, BV[...])
-    give(1, 1, 1)
     finish(0, 1)
-    copies = share(BY, y, along_y, 7, summed(BZ, copies, 8))
     give(1, 0, 1)
     give(1, 1, 2)
+    copies = share(BY, y, along_y, 7, summed(BZ, copies, 8))
+    give(1, 1, 3)
+    give(1, 0, 2)
     copies = share(BX, x, along_x, 14, summed(BY, copies, 8))
+    finish(1, 1)
+    give(1, 0, 3)
     finish(0, 0)
-    give(1, 0, 2)
-    give(1, 1, 3)
     BM[...] = summed(BX, copies, 4) * (65536.0**-0.5)
     BT[c] = BM[...]
     last = remote(BM, BT.at[c], b_send.at[17], b_recv.at[17], partner)
-    give(1, 0, 3)
-    finish(1, 1)
     finish(1, 0)
     for gi in range(2):
         ks[gi].wait_recv()
         gk[:, cols((2 * other + gi) * 128, 128)] = KR[gi, :, 0:128]
         gv[:, cols((2 * other + gi) * 128, 128)] = KR[gi, :, 128:256]
     last.wait_recv()
+    for i in range(2):
+        bias[i * 16:i * 16 + 16, :] = BT[i, 0:16, :]
+        bias[32 + 2 * i:34 + 2 * i, :] = BT[i, 16:18, :]
     for copy in core[6:]:
         copy.wait_recv()
     for copy in outs:
@@ -390,7 +438,7 @@
         copy.wait_send()
 
 
-def stepped(q, k, v, g, lk, PR, PP, PQ):
+def stepped(q, k, v, g, plan, first):
     dma = pltpu.SemaphoreType.DMA
     return pl.pallas_call(
         step_kernel,
@@ -399,15 +447,19 @@
             jax.ShapeDtypeStruct((128, 4096), BF16),
             jax.ShapeDtypeStruct((128, 512), BF16),
             jax.ShapeDtypeStruct((128, 512), BF16),
-            jax.ShapeDtypeStruct((2, 24, 128), F32),
+            jax.ShapeDtypeStruct((36, 128), F32),
         ),
-        in_specs=[ANY] * 4 + [VMEM] * 4,
+        in_specs=[HBM] * 4 + [VMEM] * 2,
         out_specs=(ANY, ANY, VMEM, VMEM, VMEM),
         scratch_shapes=[
             pltpu.VMEM((2, 2, 8, 256, 256), BF16),
             pltpu.VMEM((256, 2048), BF16),
             pltpu.VMEM((256, 2048), BF16),
             pltpu.VMEM((32, 1, 128), jnp.int32),
+            pltpu.VMEM((32, 128), jnp.int32),
+            pltpu.VMEM((32, 256), jnp.int32),
+            pltpu.VMEM((32, 128), jnp.int32),
+            pltpu.VMEM((2, 24, 128), F32),
             pltpu.VMEM((544, 2048), BF16),
             pltpu.VMEM((544, 2048), BF16),
             pltpu.VMEM((512, 2048), BF16),
@@ -426,37 +478,50 @@
             pltpu.VMEM((8, 24, 128), F32),
             pltpu.VMEM((4, 24, 128), F32),
             pltpu.VMEM((24, 128), F32),
-            dma((6,)), dma((6,)), dma((6,)), dma((2,)), dma((2,)), dma((4, 2, 4)), dma((4, 2, 4)), dma((31,)), dma((31,)),
+            dma((6,)), dma((6,)), dma((6,)), dma((2,)), dma((2,)), dma((4, 2, 4)), dma((4, 2, 4)), dma((9,)), dma((9,)),
             dma((2,)), dma((2,)), dma((2,)), dma((2,)), dma((2,)), dma((2,)), dma((2,)), dma((4, 2, 4)), dma((4, 2, 4)),
             dma((18,)), dma((18,)),
         ],
-        compiler_params=pltpu.CompilerParams(collective_id=0, has_side_effects=True, vmem_limit_bytes=62 * 2**20),
+        compiler_params=pltpu.CompilerParams(collective_id=0, has_side_effects=True, vmem_limit_bytes=LIMIT * 2**20),
         name="step",
-    )(q, k, v, g, lk, PR, PP, PQ)
+    )(q, k, v, g, plan, first)
+
+
+def place_kernel(*refs):
+    kept, (arrive, leave) = refs[10:15], refs[15:]
+    for way, sem in ((0, arrive), (1, leave)):
+        copies = []
+        for i in range(5):
+            pair = (refs[i], kept[i]) if way == 0 else (kept[i], refs[i + 5])
+            copies.append(pltpu.make_async_copy(pair[0], pair[1], sem.at[i]))
+        if way == 0:
+            for copy in copies:
+                copy.start()
+            first = copies
+        else:
+            for i in range(5):
+                first[i].wait()
+                copies[i].start()
+            for copy in copies:
+                copy.wait()
+
+
+def placed(*values):
+    return pl.pallas_call(
+        place_kernel,
+        out_shape=tuple(jax.ShapeDtypeStruct(value.shape, value.dtype) for value in values),
+        in_specs=[HBM] * 5,
+        out_specs=(HBM,) * 5,
+        scratch_shapes=[pltpu.VMEM(value.shape, value.dtype) for value in values] + [pltpu.SemaphoreType.DMA((5,))] * 2,
+        compiler_params=pltpu.CompilerParams(vmem_limit_bytes=LIMIT * 2**20),
+        name="place",
+    )(*values)
 
 
 def local(query_rows, key_rows, value_rows, out_grad, destination, group_first):
-    ctx = lax.axis_index("ctx")
-    linked = (group_first[0, 0] < ctx).astype(jnp.int32)
-    lk = jnp.broadcast_to(linked, (1, 1, 128))
-    plan = destination.reshape(32, 128)
-    blocks = plan // 128
-    spots = plan % 128
-    ids = jnp.arange(128)
-    same = (blocks[:, :, None] == blocks[:, None, :]) & (ids[None, :, None] < ids[None, None, :])
-    ranks = jnp.sum(same.astype(jnp.int32), axis=1)
-    code = blocks * 8 + ranks
-    hits = code[:, :, None] == jnp.arange(256)[None, None, :]
-    PP = jnp.sum(jnp.where(hits, spots[:, :, None] + 1, 0), axis=1)
-    PP = PP.reshape(32, 32, 8).transpose(1, 0, 2).reshape(32, 1, 256)
-    cores = (jnp.arange(32) % 2)[:, None] * 8
-    PR = (blocks * 16 + cores + ranks).reshape(16, 1, 256)
-    chip = ctx // 2
-    mine = lax.dynamic_slice_in_dim(PP.reshape(32, 16, 16), chip, 1, 1)
-    PQ = jnp.broadcast_to(jnp.where(mine == 0, 127, mine - 1), (32, 8, 16)).reshape(32, 1, 128)
-    att, gq, gk, gv, BT = stepped(query_rows, key_rows, value_rows, out_grad, lk, PR, PP, PQ)
-    bias = jnp.concatenate([BT[:, :16].reshape(4096), BT[:, 16:18].reshape(512)])
-    return att, gq, gk, gv, bias
+    outs = stepped(query_rows, key_rows, value_rows, out_grad, destination.reshape(32, 128), group_first)
+    att, gq, gk, gv, bias = placed(*outs)
+    return att, gq, gk, gv, bias.reshape(4608)
 
 
 def solution(mesh):

time: 132 us -> 120 us (0.909)
  local copies, waits for them, and re-layouts: 8.3 us -> 0 us
  other arithmetic: 4.98 us -> 0 us
    unnamed x12 -> x0, local copies, waits for them, and re-layouts: 4.7 us -> none
    pallas_call x0 -> x1, Pallas kernels: none -> 2.7 us  [placed(): pl.pallas_call(place_kernel, out_shape=tuple((jax.ShapeDtypeStruct(value....]
    reduce_sum x2 -> x0, other arithmetic: 2.11 us -> none  [the longest x1 1.4 us: local(): PP = jnp.sum(jnp.where(hits, spots[:, :, None] + 1, 0), axis=1)]
    add x2 -> x0, other arithmetic: 1.44 us -> none  [the longest x1 0.74 us: local(): code = blocks * 8 + ranks]
    slice x2 -> x0, local copies, waits for them, and re-layouts: 1.42 us -> none  [the longest x1 0.72 us: local(): BT[:, :16].reshape(4096)]
    pallas_call x1, Pallas kernels: 117 us -> 116 us  [stepped(): pl.pallas_call(step_kernel, out_shape=(jax.ShapeDtypeStruct((128, 4096),...]
    reshape x2 -> x0, local copies, waits for them, and re-layouts: 1.37 us -> none  [the longest x1 0.69 us: local(): PP = PP.reshape(32, 32, 8).transpose(1, 0, 2).reshape(32, 1, 256)]
where the time goes in v3:
time: 120 us
  Pallas kernels  118 us (98%)
  between operations  1.47 us (1%)
    pallas_call x1, Pallas kernels, stepped(): pl.pallas_call(step_kernel, out_shape=(jax.ShapeDtypeStruct((128, 4096),...  116 us
    pallas_call x1, Pallas kernels, placed(): pl.pallas_call(place_kernel, out_shape=tuple((jax.ShapeDtypeStruct(value....  2.7 us

profile of v3, /device:TPU:1, one launch (start us, length us, event | category | flops | bytes accessed | tf_op | source)
XLA Modules:
  0.0 119.8 jit_solution(5641614973957212625)
XLA Ops:
  1.3 115.6 %step.1 = (bf16[128,4096]{1,0:T(8,128)(2,1)}, bf16[128,4096]{1,0:T(8,128)(2,1)}, bf16[128,512]{1,0:T(8,128)(2,1)}, bf16[128,512]{1,0:T(8,128)(2,1)}, f32[36,128]{1,0:T(8,128)}) custom-call(bf16[128,4096]{1,0:T(8,128)(2,1)} %q.1, bf16[128,512]{1,0:T(8,128)(2,1)} %k.1, bf16[128,512]{1,0:T(8,128)(2,1)} %v.1, bf16[128,4096]{1,0:T(8,128)(2,1)} %g.1, ...), custom_call_target="tpu_custom_call" | custom-call | tf_op jit(solution)/shard_map/step/pallas_call | solution.py:443
  116.9 2.7 %place.1 = (bf16[128,4096]{1,0:T(8,128)(2,1)}, bf16[128,4096]{1,0:T(8,128)(2,1)}, bf16[128,512]{1,0:T(8,128)(2,1)}, bf16[128,512]{1,0:T(8,128)(2,1)}, f32[36,128]{1,0:T(8,128)}) custom-call(bf16[128,4096]{1,0:T(8,128)(2,1)} %get-tuple-element.15.refs_0_, bf16[128,4096]{1,0:T(8,128)(2,1)} %get-tuple-element.16.refs_1_, ...), custom_call_target="tpu_custom_call" | custom-call | tf_op jit(solution)/shard_map/place/pallas_call | solution.py:510

commit v4 on v3

--- a/solution.py
+++ b/solution.py
@@ -38,9 +38,9 @@
 
 
 def step_kernel(q, k, v, g, plan, first, att, gq, gk, gv, bias,
-                KV, QX, GX, LK, PS, PP, PQ, BT, QP, GP, OP, DQP, PAD, D, ATT, GQ, BV, R, YS, YR, KS, KR, BZ, BY, BX, BM,
+                KV, QX, GX, LK, PS, PP, PQ, BT, QP, GP, OP, DQP, PAD, D, ATT, GQ, BV, R, YS, YR, KS, KR, BZ, BY, BX, BM, YX,
                 local_sem, core_send, core_recv, y_send, y_recv, z_send, z_recv, l_send, l_recv,
-                out_sem, o_send, o_recv, k_send, k_recv, v_send, v_recv, r_send, r_recv, b_send, b_recv):
+                out_sem, o_send, o_recv, k_send, k_recv, v_send, v_recv, r_send, r_recv, b_send, b_recv, j_send, j_recv, x_send, x_recv):
     dp, ctx, yh, z, c = places()
     yl, x = dp // 4, lax.rem(dp, 4)
     y = yh * 4 + yl
@@ -146,30 +146,46 @@
 
     rows = {}
     ys = {}
+    jumps = {}
 
     def bring(gi, far, s, later=False):
         item = 2 * far + gi
-        if s == 0:
-            if far:
-                ys[gi].wait_recv()
-            else:
-                for i in (2 * gi, 2 * gi + 1):
-                    local[i].wait()
-                    core[i].wait_recv()
+        if s == 0 and far:
+            ys[gi].wait_recv()
+        elif s == 0:
+            for i in (2 * gi, 2 * gi + 1):
+                core[i].wait_recv()
+        if far and s == 4:
+            jumps[gi].wait_recv()
         for way in range(2):
-            if s > 0:
+            if 0 < s < 5 - far:
                 rows[(item, way, s - 1)].wait_recv()
-            if s < 4:
+                if s == 1 and not far:
+                    rows[(item, way, 4)].wait_recv()
+            if s < 4 - far:
                 ref = KV.at[gi, side(far), ring(z - s if way == 0 else z + s)]
                 if s == 3:
                     ref = ref.at[half[way], :]
+                elif s == 0 and not far:
+                    ref = ref.at[theirs, :]
                 rows[(item, way, s)] = remote(ref, ref, z_send.at[item, way, s], z_recv.at[item, way, s],
                                               right if way == 0 else left)
         if s == 0 and not far:
             ref = KV.at[gi, yh, z]
             ys[gi] = remote(ref, ref, y_send.at[gi], y_recv.at[gi], across)
+        if s == 4 and not far:
+            ref = KV.at[gi, yh, ring(z + 4)]
+            jumps[gi] = remote(ref, ref, j_send.at[gi], j_recv.at[gi], across)
         if not later:
             widen(gi, far, [ring(z + s)] if s in (0, 4) else [ring(z - s), ring(z + s)])
+
+    def lead(gi):
+        for i in (2 * gi, 2 * gi + 1):
+            local[i].wait()
+        ref = KV.at[gi, yh, z, mine, :]
+        for way in range(2):
+            rows[(gi, way, 4)] = remote(ref, ref, z_send.at[gi, way, 4], z_recv.at[gi, way, 4],
+                                        right if way == 0 else left)
 
     def queries(ref, gi, b):
         at = slice(b * 16 + 16, b * 16 + 32)
@@ -264,8 +280,13 @@
             term = D.at[gi, side(far), ring(target)]
             dst = R.at[item, way, s]
             if s == 0:
-                src = term.at[half[way], :]
+                if way == 0:
+                    jumps[gi].wait_recv()
+                    YX[gi] = (YX[gi].astype(F32) + term[...].astype(F32)).astype(BF16)
+                src = YX.at[gi, half[way], :]
                 dst = dst.at[half[way], :]
+            elif far and s == 1:
+                src = term
             else:
                 back[(item, way, s - 1)].wait_recv()
                 src = R.at[item, way, s - 1]
@@ -299,16 +320,17 @@
         gv[:, cols((2 * c + gi) * 128, 128)] = done[:, 128:256]
 
     def start_reduce(gi):
-        narrow(gi, [(1, ring(z + 4)), (0, ring(z + 4))])
-        give(gi, 1, 0)
-        give(gi, 0, 0)
-        narrow(gi, [(far, ring(z + i)) for i in (3, 5) for far in (1, 0)])
+        narrow(gi, [(1, ring(z + 4)), (1, ring(z + 3)), (1, ring(z + 5))])
+        jumps[gi] = remote(D.at[gi, side(1), ring(z + 4)], YX.at[gi], x_send.at[gi], x_recv.at[gi], across)
+        give(gi, 1, 1)
         narrow(gi, [(far, ring(z + i)) for i in (2, 6) for far in (1, 0)])
-        narrow(gi, [(far, ring(z + i)) for i in (1, 7) for far in (1, 0)])
-        narrow(gi, [(far, z) for far in (1, 0)])
+        narrow(gi, [(1, ring(z + 1)), (1, ring(z + 7)), (0, ring(z + 4)), (0, ring(z + 3)), (0, ring(z + 5))])
+        narrow(gi, [(0, ring(z + 1)), (0, ring(z + 7)), (1, z), (0, z)])
 
     ks = []
 
+    lead(0)
+    lead(1)
     bring(0, 0, 0, later=True)
     bring(1, 0, 0, later=True)
     flags = [remote(LK.at[flag], LK.at[flag], l_send.at[i], l_recv.at[i], along_z[i]) for i in range(7)]
@@ -339,46 +361,44 @@
     for j in range(4):
         spread(GP, GX, j)
     bring(1, 0, 1)
-    bring(0, 1, 0)
     for j in range(4, 8):
         spread(QP, QX, j)
+    bring(0, 0, 2)
+    bring(0, 1, 0)
     flag_y.wait_recv()
     part = pl.ds(c * 16, 16)
     flag_core = remote(LK.at[part], LK.at[part], l_send.at[8], l_recv.at[8], partner)
-    bring(0, 0, 2)
     for j in range(4, 8):
         spread(GP, GX, j)
+    bring(0, 0, 3)
     bring(0, 1, 1)
-    bring(0, 0, 3)
+    bring(0, 0, 4)
+    bring(1, 0, 2)
     bring(0, 1, 2)
+    flag_core.wait_recv()
+    bring(1, 0, 3)
+    bring(0, 1, 3)
     bring(1, 1, 0)
-    bring(0, 1, 3)
-    bring(1, 0, 2)
-    flag_core.wait_recv()
-    bring(0, 0, 4)
     bring(0, 1, 4)
+    bring(1, 0, 4)
+    carry = blocks(0, 0, opening())
     bring(1, 1, 1)
-    carry = blocks(0, 0, opening())
-    bring(1, 0, 3)
     carry = blocks(0, 1, carry)
+    carry = blocks(0, 2, carry)
     bring(1, 1, 2)
-    carry = blocks(0, 2, carry)
-    bring(1, 0, 4)
     carry = blocks(0, 3, carry)
+    start_reduce(0)
     bring(1, 1, 3)
-    start_reduce(0)
     bring(1, 1, 4)
-    give(0, 1, 1)
-    give(0, 0, 1)
     carry = blocks(1, 0, opening())
     give(0, 1, 2)
     carry = blocks(1, 1, carry)
-    give(0, 0, 2)
     carry = blocks(1, 2, carry)
     give(0, 1, 3)
+    give(0, 0, 0)
     carry = blocks(1, 3, carry)
     start_reduce(1)
-    give(0, 0, 3)
+    give(0, 0, 1)
     here = placing(chip)
     for j in range(8):
         at = slice(j * 256, (j + 1) * 256)
@@ -388,7 +408,6 @@
         sums = jnp.sum(wide, axis=0, keepdims=True)
         BV[2 * j:2 * j + 1, :] = sums[:, 0:128]
         BV[2 * j + 1:2 * j + 2, :] = sums[:, 128:256]
-    give(1, 1, 1)
     outs = []
     for i, (src, dst) in enumerate(((ATT, att), (GQ, gq))):
         outs.append(copied(src.at[mine, :], dst.at[:, cols(c * 2048, 2048)], out_sem.at[i]))
@@ -408,20 +427,23 @@
         return value
 
     copies = share(BZ, z, along_z, 0, BV[...])
+    give(1, 1, 2)
     finish(0, 1)
+    give(0, 0, 2)
+    copies = share(BY, y, along_y, 7, summed(BZ, copies, 8))
+    give(1, 0, 0)
+    give(1, 1, 3)
     give(1, 0, 1)
-    give(1, 1, 2)
-    copies = share(BY, y, along_y, 7, summed(BZ, copies, 8))
-    give(1, 1, 3)
+    give(0, 0, 3)
+    finish(1, 1)
     give(1, 0, 2)
     copies = share(BX, x, along_x, 14, summed(BY, copies, 8))
-    finish(1, 1)
+    finish(0, 0)
     give(1, 0, 3)
-    finish(0, 0)
+    finish(1, 0)
     BM[...] = summed(BX, copies, 4) * (65536.0**-0.5)
     BT[c] = BM[...]
     last = remote(BM, BT.at[c], b_send.at[17], b_recv.at[17], partner)
-    finish(1, 0)
     for gi in range(2):
         ks[gi].wait_recv()
         gk[:, cols((2 * other + gi) * 128, 128)] = KR[gi, :, 0:128]
@@ -478,9 +500,10 @@
             pltpu.VMEM((8, 24, 128), F32),
             pltpu.VMEM((4, 24, 128), F32),
             pltpu.VMEM((24, 128), F32),
-            dma((6,)), dma((6,)), dma((6,)), dma((2,)), dma((2,)), dma((4, 2, 4)), dma((4, 2, 4)), dma((9,)), dma((9,)),
+            pltpu.VMEM((2, 256, 256), BF16),
+            dma((6,)), dma((6,)), dma((6,)), dma((2,)), dma((2,)), dma((4, 2, 5)), dma((4, 2, 5)), dma((9,)), dma((9,)),
             dma((2,)), dma((2,)), dma((2,)), dma((2,)), dma((2,)), dma((2,)), dma((2,)), dma((4, 2, 4)), dma((4, 2, 4)),
-            dma((18,)), dma((18,)),
+            dma((18,)), dma((18,)), dma((2,)), dma((2,)), dma((2,)), dma((2,)),
         ],
         compiler_params=pltpu.CompilerParams(collective_id=0, has_side_effects=True, vmem_limit_bytes=LIMIT * 2**20),
         name="step",

time: 120 us -> 114 us (0.950)
  Pallas kernels: 118 us -> 112 us
    pallas_call x1, Pallas kernels: 116 us -> 109 us  [stepped(): pl.pallas_call(step_kernel, out_shape=(jax.ShapeDtypeStruct((128, 4096),...]
where the time goes in v4:
time: 114 us
  Pallas kernels  112 us (98%)
  between operations  1.47 us (1%)
    pallas_call x1, Pallas kernels, stepped(): pl.pallas_call(step_kernel, out_shape=(jax.ShapeDtypeStruct((128, 4096),...  109 us
    pallas_call x1, Pallas kernels, placed(): pl.pallas_call(place_kernel, out_shape=tuple((jax.ShapeDtypeStruct(value....  2.7 us

profile of v4, /device:TPU:1, one launch (start us, length us, event | category | flops | bytes accessed | tf_op | source)
XLA Modules:
  0.0 113.6 jit_solution(434090860896516376)
XLA Ops:
  1.3 109.4 %step.1 = (bf16[128,4096]{1,0:T(8,128)(2,1)}, bf16[128,4096]{1,0:T(8,128)(2,1)}, bf16[128,512]{1,0:T(8,128)(2,1)}, bf16[128,512]{1,0:T(8,128)(2,1)}, f32[36,128]{1,0:T(8,128)}) custom-call(bf16[128,4096]{1,0:T(8,128)(2,1)} %q.1, bf16[128,512]{1,0:T(8,128)(2,1)} %k.1, bf16[128,512]{1,0:T(8,128)(2,1)} %v.1, bf16[128,4096]{1,0:T(8,128)(2,1)} %g.1, ...), custom_call_target="tpu_custom_call" | custom-call | tf_op jit(solution)/shard_map/step/pallas_call | solution.py:465
  110.7 2.7 %place.1 = (bf16[128,4096]{1,0:T(8,128)(2,1)}, bf16[128,4096]{1,0:T(8,128)(2,1)}, bf16[128,512]{1,0:T(8,128)(2,1)}, bf16[128,512]{1,0:T(8,128)(2,1)}, f32[36,128]{1,0:T(8,128)}) custom-call(bf16[128,4096]{1,0:T(8,128)(2,1)} %get-tuple-element.15.refs_0_, bf16[128,4096]{1,0:T(8,128)(2,1)} %get-tuple-element.16.refs_1_, ...), custom_call_target="tpu_custom_call" | custom-call | tf_op jit(solution)/shard_map/place/pallas_call | solution.py:533

commit v5 on v4

--- a/solution.py
+++ b/solution.py
@@ -157,19 +157,14 @@
                 core[i].wait_recv()
         if far and s == 4:
             jumps[gi].wait_recv()
-        for way in range(2):
-            if 0 < s < 5 - far:
-                rows[(item, way, s - 1)].wait_recv()
-                if s == 1 and not far:
-                    rows[(item, way, 4)].wait_recv()
-            if s < 4 - far:
-                ref = KV.at[gi, side(far), ring(z - s if way == 0 else z + s)]
-                if s == 3:
-                    ref = ref.at[half[way], :]
-                elif s == 0 and not far:
-                    ref = ref.at[theirs, :]
-                rows[(item, way, s)] = remote(ref, ref, z_send.at[item, way, s], z_recv.at[item, way, s],
-                                              right if way == 0 else left)
+        for part in range(2):
+            for way in range(2):
+                if 0 < s < 5 - far and (s < 4 or part == way):
+                    rows[(item, way, s - 1, part)].wait_recv()
+                if s < 4 - far and (s < 3 or part == way) and (s or far or part):
+                    ref = KV.at[gi, side(far), ring(z - s if way == 0 else z + s), (mine, theirs)[part], :]
+                    rows[(item, way, s, part)] = remote(ref, ref, z_send.at[item, way, s, part],
+                                                        z_recv.at[item, way, s, part], right if way == 0 else left)
         if s == 0 and not far:
             ref = KV.at[gi, yh, z]
             ys[gi] = remote(ref, ref, y_send.at[gi], y_recv.at[gi], across)
@@ -184,8 +179,8 @@
             local[i].wait()
         ref = KV.at[gi, yh, z, mine, :]
         for way in range(2):
-            rows[(gi, way, 4)] = remote(ref, ref, z_send.at[gi, way, 4], z_recv.at[gi, way, 4],
-                                        right if way == 0 else left)
+            rows[(gi, way, 0, 0)] = remote(ref, ref, z_send.at[gi, way, 0, 0], z_recv.at[gi, way, 0, 0],
+                                           right if way == 0 else left)
 
     def queries(ref, gi, b):
         at = slice(b * 16 + 16, b * 16 + 32)
@@ -275,29 +270,25 @@
 
     def give(gi, far, s):
         item = 2 * far + gi
-        for way in range(2):
-            target = z + 4 - s if way == 0 else z - 4 + s
-            term = D.at[gi, side(far), ring(target)]
-            dst = R.at[item, way, s]
-            if s == 0:
-                if way == 0:
-                    jumps[gi].wait_recv()
-                    YX[gi] = (YX[gi].astype(F32) + term[...].astype(F32)).astype(BF16)
-                src = YX.at[gi, half[way], :]
-                dst = dst.at[half[way], :]
-            elif far and s == 1:
-                src = term
-            else:
-                back[(item, way, s - 1)].wait_recv()
-                src = R.at[item, way, s - 1]
-                for part in range(2):
-                    at = slice(part * 128, part * 128 + 128)
-                    if s == 1 and part != way:
-                        src[at, :] = term[at, :]
-                    else:
-                        src[at, :] = (src[at, :].astype(F32) + term[at, :].astype(F32)).astype(BF16)
-            back[(item, way, s)] = remote(src, dst, r_send.at[item, way, s], r_recv.at[item, way, s],
-                                          right if way == 0 else left)
+        if s == 0:
+            jumps[gi].wait_recv()
+            YX[gi] = (YX[gi].astype(F32) + D[gi, side(0), ring(z + 4)].astype(F32)).astype(BF16)
+        for part in range(2):
+            for way in range(2):
+                at = half[part]
+                term = D.at[gi, side(far), ring(z + 4 - s if way == 0 else z - 4 + s), at, :]
+                if s == 0:
+                    if part != way:
+                        continue
+                    src = YX.at[gi, at, :]
+                elif s == 1 and (far or part != way):
+                    src = term
+                else:
+                    back[(item, way, s - 1, part)].wait_recv()
+                    src = R.at[item, way, s - 1, at, :]
+                    src[...] = (src[...].astype(F32) + term[...].astype(F32)).astype(BF16)
+                back[(item, way, s, part)] = remote(src, R.at[item, way, s, at, :], r_send.at[item, way, s, part],
+                                                    r_recv.at[item, way, s, part], right if way == 0 else left)
 
     def total(gi, far, at):
         item = 2 * far + gi
@@ -306,8 +297,9 @@
 
     def finish(gi, far):
         item = 2 * far + gi
-        back[(item, 0, 3)].wait_recv()
-        back[(item, 1, 3)].wait_recv()
+        for way in range(2):
+            for part in range(2):
+                back[(item, way, 3, part)].wait_recv()
         if far:
             YS[gi] = total(gi, 1, slice(0, 256)).astype(BF16)
             ys[gi] = remote(YS.at[gi], YR.at[gi], v_send.at[gi], v_recv.at[gi], across)
@@ -501,8 +493,8 @@
             pltpu.VMEM((4, 24, 128), F32),
             pltpu.VMEM((24, 128), F32),
             pltpu.VMEM((2, 256, 256), BF16),
-            dma((6,)), dma((6,)), dma((6,)), dma((2,)), dma((2,)), dma((4, 2, 5)), dma((4, 2, 5)), dma((9,)), dma((9,)),
-            dma((2,)), dma((2,)), dma((2,)), dma((2,)), dma((2,)), dma((2,)), dma((2,)), dma((4, 2, 4)), dma((4, 2, 4)),
+            dma((6,)), dma((6,)), dma((6,)), dma((2,)), dma((2,)), dma((4, 2, 4, 2)), dma((4, 2, 4, 2)), dma((9,)), dma((9,)),
+            dma((2,)), dma((2,)), dma((2,)), dma((2,)), dma((2,)), dma((2,)), dma((2,)), dma((4, 2, 4, 2)), dma((4, 2, 4, 2)),
             dma((18,)), dma((18,)), dma((2,)), dma((2,)), dma((2,)), dma((2,)),
         ],
         compiler_params=pltpu.CompilerParams(collective_id=0, has_side_effects=True, vmem_limit_bytes=LIMIT * 2**20),

time: 114 us -> 112 us (0.982)
  Pallas kernels: 112 us -> 110 us
    pallas_call x1, Pallas kernels: 109 us -> 107 us  [stepped(): pl.pallas_call(step_kernel, out_shape=(jax.ShapeDtypeStruct((128, 4096),...]
where the time goes in v5:
time: 112 us; the launch traced here: 111 us
  Pallas kernels  110 us (98%)
  between operations  1.47 us (1%)
    pallas_call x1, Pallas kernels, stepped(): pl.pallas_call(step_kernel, out_shape=(jax.ShapeDtypeStruct((128, 4096),...  107 us
    pallas_call x1, Pallas kernels, placed(): pl.pallas_call(place_kernel, out_shape=tuple((jax.ShapeDtypeStruct(value....  2.7 us

profile of v5, /device:TPU:1, one launch (start us, length us, event | category | flops | bytes accessed | tf_op | source)
XLA Modules:
  0.0 111.4 jit_solution(14327184735086426064)
XLA Ops:
  1.3 107.2 %step.1 = (bf16[128,4096]{1,0:T(8,128)(2,1)}, bf16[128,4096]{1,0:T(8,128)(2,1)}, bf16[128,512]{1,0:T(8,128)(2,1)}, bf16[128,512]{1,0:T(8,128)(2,1)}, f32[36,128]{1,0:T(8,128)}) custom-call(bf16[128,4096]{1,0:T(8,128)(2,1)} %q.1, bf16[128,512]{1,0:T(8,128)(2,1)} %k.1, bf16[128,512]{1,0:T(8,128)(2,1)} %v.1, bf16[128,4096]{1,0:T(8,128)(2,1)} %g.1, ...), custom_call_target="tpu_custom_call" | custom-call | tf_op jit(solution)/shard_map/step/pallas_call | solution.py:457
  108.5 2.7 %place.1 = (bf16[128,4096]{1,0:T(8,128)(2,1)}, bf16[128,4096]{1,0:T(8,128)(2,1)}, bf16[128,512]{1,0:T(8,128)(2,1)}, bf16[128,512]{1,0:T(8,128)(2,1)}, f32[36,128]{1,0:T(8,128)}) custom-call(bf16[128,4096]{1,0:T(8,128)(2,1)} %get-tuple-element.15.refs_0_, bf16[128,4096]{1,0:T(8,128)(2,1)} %get-tuple-element.16.refs_1_, ...), custom_call_target="tpu_custom_call" | custom-call | tf_op jit(solution)/shard_map/place/pallas_call | solution.py:525
